TPU v7x, 128 devices: a whole 4x4x4 slice. The times are simulated.
128 devices in a mesh: gx: 8 (over y, core), gy: 16 (over z, x).
Axes of the slice: x: 4, y: 4, z: 4, core: 2. Of those that a mesh axis runs over, the one named last changes fastest.
Arguments:
- transfer: bfloat16 [2048, 75, 128], P(('gx', 'gy')), may hold values from -6 to 6
- positions: float32 [2048, 3, 128], P(('gx', 'gy')), may hold values from -4 to 4
- normals: float32 [2048, 3, 128], P(('gx', 'gy')), may hold values from -4 to 4
- area: float32 [2048, 128], P(('gx', 'gy')), may hold values from 0.06 to 3
- albedo: float32 [2048, 3, 128], P(('gx', 'gy')), may hold values from 0.3 to 0.9
- pairs: int32 [2048, 40], P(('gx', 'gy')), may hold values from 0 to 2047, as said below
- home: int32 [2048], replicated, may hold values from 0 to 2047, as said below
Outputs:
- bounce_one: bfloat16 [2048, 75, 128], P(('gx', 'gy'))
- bounce_two: bfloat16 [2048, 75, 128], P(('gx', 'gy'))
- energies: float32 [2], replicated
Inputs may be any that keep to these rules, and one draw needn't show every extreme that they name: `home`: A permutation; the block in slot s is held by device s // 16, devices counted gx major. `pairs`: the first 16 entries of a row name blocks held by the same device as the row's slot, the other 24 name blocks held by other devices. Over the rows of one device, the far entries name at most 2 distinct blocks of any one other device, and exactly 2 of some. Ids may repeat within a row; each entry counts.
All inputs are finite; a program needn't handle non-finite values.
Results may differ from a plain program's by a relative error of at most 0.02.
Values may be sent and summed in bfloat16 or wider, within the bound.
No kernel may reach another device: no remote copies, remote signals or barrier semaphores. Data moves between devices by JAX's collectives and lax.ppermute only.
A program may use at most 128 MiB of HBM per device.

v0:
```python
import functools
import math

import jax
import jax.numpy as jnp
from jax import lax
from jax.experimental import pallas as pl
from jax.experimental.pallas import tpu as pltpu
from jax.sharding import Mesh
from jax.sharding import PartitionSpec as P

COLORS = 3
NEAR = 16
FAR = 24
PAIRS = NEAR + FAR
CAP = 2
CH = 75
CHP = 80
BLK = 16
VERT = 128
DEVS = 128
ROWS = DEVS * CAP
AXES = ("gx_0", "gx_1", "gy_0", "gy_1")
CHUNK = 32

F32 = jnp.float32
BF16 = jnp.bfloat16
I32 = jnp.int32


def params(limit_mib=24):
    return pltpu.CompilerParams(
        dimension_semantics=("arbitrary",), vmem_limit_bytes=limit_mib * 1024 * 1024
    )


def cost(flops, read=0):
    return pl.CostEstimate(flops=int(flops), bytes_accessed=int(read), transcendentals=0)


def index_kernel(pairs_ref, home_ref, idx_ref, req_ref):
    home = home_ref[...]
    both = jnp.concatenate([home >> 4, home & 15], axis=0).astype(F32).astype(BF16)
    pairs = pairs_ref[...]
    low = pairs & 127
    high = pairs >> 7
    sub = lax.broadcasted_iota(I32, (VERT, PAIRS), 0)
    sub_f = sub.astype(F32)
    sub16 = lax.broadcasted_iota(I32, (16, PAIRS), 0)
    lane = lax.broadcasted_iota(I32, (VERT, PAIRS), 1)
    lane_row = lax.broadcasted_iota(I32, (1, PAIRS), 1)
    is_far = lane >= NEAR
    owners, locals_ = [], []
    least = jnp.full((VERT, PAIRS), 99.0, F32)
    most = jnp.full((VERT, PAIRS), -1.0, F32)
    for s in range(BLK):
        hot = jnp.where(sub == low[s : s + 1, :], 1.0, 0.0).astype(BF16)
        got = jnp.dot(both, hot, preferred_element_type=F32)
        here = sub16 == high[s : s + 1, :]
        owner = jnp.sum(jnp.where(here, got[:16], 0.0), axis=0, keepdims=True)
        local = jnp.sum(jnp.where(here, got[16:], 0.0), axis=0, keepdims=True)
        owners.append(owner)
        locals_.append(local)
        same = (sub_f == owner) & is_far
        least = jnp.minimum(least, jnp.where(same, local, 99.0))
        most = jnp.maximum(most, jnp.where(same, local, -1.0))
    lo = jnp.min(least, axis=1, keepdims=True)
    hi = jnp.max(most, axis=1, keepdims=True)
    for s in range(BLK):
        first = jnp.sum(jnp.where(sub_f == owners[s], lo, 0.0), axis=0, keepdims=True)
        far_row = owners[s] * 2.0 + jnp.where(locals_[s] == first, 0.0, 1.0)
        idx_ref[s : s + 1, :] = jnp.where(lane_row < NEAR, locals_[s], far_row).astype(I32)
    used = hi >= 0.0
    req_ref[:, 0:1] = jnp.where(used, lo, 0.0).astype(I32)
    req_ref[:, 1:2] = jnp.where(used, hi, 0.0).astype(I32)


def find_indices(pairs, home):
    return pl.pallas_call(
        index_kernel,
        out_shape=(
            jax.ShapeDtypeStruct((BLK, PAIRS), I32),
            jax.ShapeDtypeStruct((DEVS, CAP), I32),
        ),
        cost_estimate=cost(4e6),
        compiler_params=pltpu.CompilerParams(vmem_limit_bytes=8 * 1024 * 1024),
        name="indices",
    )(pairs, home.reshape(BLK, VERT))


def geometry_kernel(req_ref, pos_ref, nrm_ref, area_ref, out_ref, table):
    table[:, 0:3, :] = pos_ref[...]
    table[:, 3:6, :] = nrm_ref[...]
    table[:, 6:7, :] = area_ref[...]
    table[:, 7:8, :] = jnp.zeros((BLK, 1, VERT), F32)

    def put(i, carry):
        out_ref[i] = table[req_ref[i]].astype(BF16)
        return carry

    lax.fori_loop(0, ROWS, put, 0, unroll=8)


def pack_geometry(req, pos, nrm, area):
    whole = lambda *shape: pl.BlockSpec(shape, lambda i, *_: (0,) * len(shape))
    return pl.pallas_call(
        geometry_kernel,
        grid_spec=pltpu.PrefetchScalarGridSpec(
            num_scalar_prefetch=1,
            grid=(1,),
            in_specs=[whole(BLK, 3, VERT), whole(BLK, 3, VERT), whole(BLK, 1, VERT)],
            out_specs=whole(ROWS, 8, VERT),
            scratch_shapes=[pltpu.VMEM((BLK, 8, VERT), F32)],
        ),
        out_shape=jax.ShapeDtypeStruct((ROWS, 8, VERT), BF16),
        cost_estimate=cost(2e6),
        compiler_params=params(8),
        name="pack_geometry",
    )(req, pos, nrm, area)


def send_kernel(req_ref, field_ref, out_ref, slab, sem):
    slab[:, 64:, :] = jnp.zeros((BLK, CHP - 64, VERT), BF16)
    slab[:, :CH, :] = field_ref[...]

    def put(i, carry):
        pltpu.make_async_copy(slab.at[req_ref[i]], out_ref.at[i], sem).start()
        return carry

    lax.fori_loop(0, ROWS, put, 0, unroll=8)
    pltpu.make_async_copy(out_ref, out_ref, sem).wait()


def pack_field(req, field):
    return pl.pallas_call(
        send_kernel,
        grid_spec=pltpu.PrefetchScalarGridSpec(
            num_scalar_prefetch=1,
            grid=(1,),
            in_specs=[pl.BlockSpec((BLK, CH, VERT), lambda i, *_: (0, 0, 0))],
            out_specs=pl.BlockSpec(memory_space=pl.ANY),
            scratch_shapes=[pltpu.VMEM((BLK, CHP, VERT), BF16), pltpu.SemaphoreType.DMA],
        ),
        out_shape=jax.ShapeDtypeStruct((ROWS, CHP, VERT), BF16),
        cost_estimate=cost(1e7),
        compiler_params=params(8),
        name="pack_field",
    )(req, field)


def fill_tiles(index_of, count, slot_geo, table, out_ref):
    columns = slot_geo.T
    for c in range(VERT // CHUNK):
        part = columns[c * CHUNK : (c + 1) * CHUNK]
        recv = [jnp.broadcast_to(part[:, i : i + 1], (CHUNK, VERT)) for i in range(6)]

        def one(j, carry, c=c, recv=recv):
            rows = table[index_of(j)]
            gap = [rows[i : i + 1] - recv[i] for i in range(3)]
            soft = gap[0] * gap[0] + gap[1] * gap[1] + gap[2] * gap[2] + 1.0
            near = recv[3] * gap[0] + recv[4] * gap[1] + recv[5] * gap[2]
            far = rows[3:4] * gap[0] + rows[4:5] * gap[1] + rows[5:6] * gap[2]
            value = jnp.maximum(near, 0.0) * jnp.maximum(far, 0.0) / (soft * soft)
            at = pl.multiple_of(j * VERT, VERT)
            out_ref[0, c * CHUNK : (c + 1) * CHUNK, pl.ds(at, VERT)] = value.astype(BF16)
            return carry

        lax.fori_loop(0, count, one, 0, unroll=4)


def scaled(normal, area):
    return normal * (area * (-1.0 / math.pi))


def product(left, right):
    return lax.dot_general(left, right, (((1,), (1,)), ((), ())), preferred_element_type=F32)


def near_kernel(idx_ref, field_ref, pos_ref, nrm_ref, area_ref, tiles_ref, sum_ref, table, geo, rows):
    s = pl.program_id(0)

    @pl.when(s == 0)
    def _():
        table[:, 0:3, :] = pos_ref[...]
        table[:, 3:6, :] = scaled(nrm_ref[...], area_ref[...])
        table[:, 6:8, :] = jnp.zeros((BLK, 2, VERT), F32)
        geo[:, 0:3, :] = pos_ref[...]
        geo[:, 3:6, :] = nrm_ref[...]
        geo[:, 6:8, :] = jnp.zeros((BLK, 2, VERT), F32)

    fill_tiles(lambda j: idx_ref[s * PAIRS + j], NEAR, geo[s], table, tiles_ref)
    for j in range(NEAR):
        rows[:, j * VERT : (j + 1) * VERT] = field_ref[idx_ref[s * PAIRS + j]]
    sum_ref[0] = product(rows[...], tiles_ref[0])


def near_first(idx, field, pos, nrm, area):
    whole = lambda *shape: pl.BlockSpec(shape, lambda i, *_: (0,) * len(shape))
    return pl.pallas_call(
        near_kernel,
        grid_spec=pltpu.PrefetchScalarGridSpec(
            num_scalar_prefetch=1,
            grid=(BLK,),
            in_specs=[
                whole(BLK, CH, VERT),
                whole(BLK, 3, VERT),
                whole(BLK, 3, VERT),
                whole(BLK, 1, VERT),
            ],
            out_specs=[
                pl.BlockSpec((1, VERT, NEAR * VERT), lambda i, *_: (i, 0, 0)),
                pl.BlockSpec((1, CH, VERT), lambda i, *_: (i, 0, 0)),
            ],
            scratch_shapes=[
                pltpu.VMEM((BLK, 8, VERT), F32),
                pltpu.VMEM((BLK, 8, VERT), F32),
                pltpu.VMEM((CH, NEAR * VERT), BF16),
            ],
        ),
        out_shape=(
            jax.ShapeDtypeStruct((BLK, VERT, NEAR * VERT), BF16),
            jax.ShapeDtypeStruct((BLK, CH, VERT), F32),
        ),
        cost_estimate=cost(6e8),
        compiler_params=params(),
        name="near_first",
    )(idx, field, pos, nrm, area)


def near_again_kernel(idx_ref, field_ref, tiles_ref, sum_ref, rows):
    s = pl.program_id(0)
    for j in range(NEAR):
        rows[:, j * VERT : (j + 1) * VERT] = field_ref[idx_ref[s * PAIRS + j]]
    sum_ref[0] = product(rows[...], tiles_ref[0])


def near_again(idx, field, tiles):
    return pl.pallas_call(
        near_again_kernel,
        grid_spec=pltpu.PrefetchScalarGridSpec(
            num_scalar_prefetch=1,
            grid=(BLK,),
            in_specs=[
                pl.BlockSpec((BLK, CH, VERT), lambda i, *_: (0, 0, 0)),
                pl.BlockSpec((1, VERT, NEAR * VERT), lambda i, *_: (i, 0, 0)),
            ],
            out_specs=pl.BlockSpec((1, CH, VERT), lambda i, *_: (i, 0, 0)),
            scratch_shapes=[pltpu.VMEM((CH, NEAR * VERT), BF16)],
        ),
        out_shape=jax.ShapeDtypeStruct((BLK, CH, VERT), F32),
        cost_estimate=cost(3e8),
        compiler_params=params(),
        name="near_again",
    )(idx, field, tiles)


def far_tiles_kernel(idx_ref, got_ref, pos_ref, nrm_ref, tiles_ref, table, geo):
    s = pl.program_id(0)

    @pl.when(s == 0)
    def _():
        got = got_ref[...].astype(F32)
        table[:, 0:3, :] = got[:, 0:3]
        table[:, 3:6, :] = scaled(got[:, 3:6], got[:, 6:7])
        table[:, 6:8, :] = jnp.zeros((ROWS, 2, VERT), F32)
        geo[:, 0:3, :] = pos_ref[...]
        geo[:, 3:6, :] = nrm_ref[...]
        geo[:, 6:8, :] = jnp.zeros((BLK, 2, VERT), F32)

    fill_tiles(lambda j: idx_ref[s * PAIRS + NEAR + j], FAR, geo[s], table, tiles_ref)


def far_tiles(idx, got, pos, nrm):
    whole = lambda *shape: pl.BlockSpec(shape, lambda i, *_: (0,) * len(shape))
    return pl.pallas_call(
        far_tiles_kernel,
        grid_spec=pltpu.PrefetchScalarGridSpec(
            num_scalar_prefetch=1,
            grid=(BLK,),
            in_specs=[whole(ROWS, 8, VERT), whole(BLK, 3, VERT), whole(BLK, 3, VERT)],
            out_specs=pl.BlockSpec((1, VERT, FAR * VERT), lambda i, *_: (i, 0, 0)),
            scratch_shapes=[pltpu.VMEM((ROWS, 8, VERT), F32), pltpu.VMEM((BLK, 8, VERT), F32)],
        ),
        out_shape=jax.ShapeDtypeStruct((BLK, VERT, FAR * VERT), BF16),
        cost_estimate=cost(6e8),
        compiler_params=params(),
        name="far_tiles",
    )(idx, got, pos, nrm)


def far_kernel(idx_ref, got_ref, tiles_ref, near_ref, albedo_ref, area_ref, out_ref, energy_ref, rows):
    s = pl.program_id(0)
    for j in range(FAR):
        rows[:, j * VERT : (j + 1) * VERT] = got_ref[idx_ref[s * PAIRS + NEAR + j]]
    total = near_ref[0] + product(rows[...], tiles_ref[0])[:CH]
    channel = lax.broadcasted_iota(I32, (CH, VERT), 0)
    shade = jnp.where(
        channel < CH // COLORS,
        albedo_ref[0, 0:1, :],
        jnp.where(channel < 2 * (CH // COLORS), albedo_ref[0, 1:2, :], albedo_ref[0, 2:3, :]),
    )
    bounce = total * shade
    out_ref[0] = bounce.astype(BF16)
    share = jnp.sum(area_ref[0] * bounce * bounce, axis=0, keepdims=True)

    @pl.when(s == 0)
    def _():
        energy_ref[...] = share

    @pl.when(s > 0)
    def _():
        energy_ref[...] = energy_ref[...] + share


def far_bounce(idx, got, tiles, near, albedo, area):
    slot = lambda *shape: pl.BlockSpec((1,) + shape, lambda i, *_: (i, 0, 0))
    return pl.pallas_call(
        far_kernel,
        grid_spec=pltpu.PrefetchScalarGridSpec(
            num_scalar_prefetch=1,
            grid=(BLK,),
            in_specs=[
                pl.BlockSpec((ROWS, CHP, VERT), lambda i, *_: (0, 0, 0)),
                slot(VERT, FAR * VERT),
                slot(CH, VERT),
                slot(COLORS, VERT),
                slot(1, VERT),
            ],
            out_specs=[slot(CH, VERT), pl.BlockSpec((1, VERT), lambda i, *_: (0, 0))],
            scratch_shapes=[pltpu.VMEM((CHP, FAR * VERT), BF16)],
        ),
        out_shape=(
            jax.ShapeDtypeStruct((BLK, CH, VERT), BF16),
            jax.ShapeDtypeStruct((1, VERT), F32),
        ),
        cost_estimate=cost(5e8),
        compiler_params=params(),
        name="far_bounce",
    )(idx, got, tiles, near, albedo, area)


def swap(value):
    return lax.all_to_all(value, AXES, split_axis=0, concat_axis=0, tiled=True)


def body(transfer, positions, normals, area, albedo, pairs, home):
    area_row = area.reshape(BLK, 1, VERT)
    idx, need = find_indices(pairs, home)
    idx = idx.reshape(-1)
    asked = swap(need).reshape(-1)
    near_tiles, near_one = near_first(idx, transfer, positions, normals, area_row)
    geometry = swap(pack_geometry(asked, positions, normals, area_row))
    got_one = swap(pack_field(asked, transfer))
    tiles = far_tiles(idx, geometry, positions, normals)
    bounce_one, share_one = far_bounce(idx, got_one, tiles, near_one, albedo, area_row)
    got_two = swap(pack_field(asked, bounce_one))
    near_two = near_again(idx, bounce_one, near_tiles)
    bounce_two, share_two = far_bounce(idx, got_two, tiles, near_two, albedo, area_row)
    shares = jnp.concatenate([share_one, share_two], axis=0)
    shares = swap(jnp.broadcast_to(shares[None], (DEVS, 2, VERT)))
    energies = jnp.sum(shares, axis=(0, 2)) * (1.0 / (DEVS * BLK * VERT * CH))
    return bounce_one, bounce_two, energies


def solution(mesh):
    finer = Mesh(mesh.devices.reshape(4, 2, 4, 4), AXES)
    three = P(AXES, None, None)
    return jax.shard_map(
        body,
        mesh=finer,
        in_specs=(three, three, three, P(AXES, None), three, P(AXES, None), P()),
        out_specs=(three, three, P()),
        check_vma=False,
    )
```

profile of v0, /device:TPU:1, one launch (start us, length us, event | category | flops | bytes accessed | tf_op | source)
XLA Modules:
  0.0 257.9 jit_solution(13000129529272624672)
XLA Ops:
  1.3 0.7 copy-done.10
  2.0 1.3 indices.1
  3.3 11.5 %all-to-all-start = ((s32[128,1,2]{2,1,0:T(1,128)}), s32[128,1,2]{2,1,0:T(1,128)S(1)}, u32[]{:S(2)}, u32[]{:S(2)}) async-start(s32[128,1,2]{2,1,0:T(1,128)} %bitcast.2), calls=%async_computation | async-start | bytes 131072 | tf_op jit(solution)/shard_map/all_to_all | solution.py:343
  14.8 0.8 copy.62.pos_ref
  15.6 0.8 copy.63.nrm_ref
  16.3 8.2 %all-to-all-done = s32[128,1,2]{2,1,0:T(1,128)S(1)} async-done(((s32[128,1,2]{2,1,0:T(1,128)}), s32[128,1,2]{2,1,0:T(1,128)S(1)}, u32[]{:S(2)}, u32[]{:S(2)}) %all-to-all-start) | async-done | bytes 1056 | tf_op jit(solution)/shard_map/all_to_all | solution.py:343
  25.1 0.8 reduce.3
  26.7 1.8 pack_geometry.1
  28.5 4.3 %all-to-all-start.2 = ((bf16[256,8,128]{2,1,0:T(8,128)(2,1)}), bf16[256,8,128]{2,1,0:T(8,128)(2,1)S(1)}, u32[]{:S(2)}, u32[]{:S(2)}) async-start(bf16[256,8,128]{2,1,0:T(8,128)(2,1)} %pack_geometry.1), calls=%async_computation.2 | async-start | bytes 1048576 | tf_op jit(solution)/shard_map/all_to_all | solution.py:343
  32.8 1.1 copy.61.field_ref
  33.9 8.7 %pack_field.2 = bf16[256,80,128]{2,1,0:T(8,128)(2,1)S(1)} custom-call(s32[256]{0:T(256)S(1)} %reshape.24.req_ref, bf16[16,75,128]{2,1,0:T(8,128)(2,1)S(1)} %copy.61.field_ref), custom_call_target="tpu_custom_call" | custom-call | flops 10000000 | tf_op jit(solution)/shard_map/pack_field/pallas_call | solution.py:135
  42.6 2.3 copy-done.3
  44.9 2.0 all-to-all-done.2.got_ref
  47.0 8.2 %all-to-all-start.1 = ((bf16[256,80,128]{2,1,0:T(8,128)(2,1)}), bf16[256,80,128]{2,1,0:T(8,128)(2,1)}, u32[]{:S(2)}, u32[]{:S(2)}) async-start(bf16[256,80,128]{2,1,0:T(8,128)(2,1)} %copy-done.3), calls=%async_computation.1 | async-start | bytes 10485760 | tf_op jit(solution)/shard_map/all_to_all | solution.py:343
  55.3 30.4 %near_first.1 = (bf16[16,128,2048]{2,1,0:T(8,128)(2,1)S(1)}, f32[16,75,128]{2,1,0:T(8,128)S(1)}) custom-call(s32[640]{0:T(1024)S(1)} %reshape.23.idx_ref, bf16[16,75,128]{2,1,0:T(8,128)(2,1)S(1)} %copy.61.field_ref, f32[16,3,128]{2,1,0:T(4,128)S(1)} %copy.62.pos_ref, f32[16,3,128]{2,1,0:T(4,128)S(1)} %copy.63.nrm_ref, f32[16,1,128]{2,1,0:T(1,128)S(1)} %bitcast.6), custom_call_target="tpu_custom_call" | custom-call | flops 600000000 | tf_op jit(solution)/shard_map/near_first/pallas_call | solution.py:199
  85.7 3.2 %copy-done.5 = bf16[16,128,2048]{2,1,0:T(8,128)(2,1)} copy-done((bf16[16,128,2048]{2,1,0:T(8,128)(2,1)}, bf16[16,128,2048]{2,1,0:T(8,128)(2,1)S(1)}, u32[]{:S(2)}) %copy-start.5) | copy-done | bytes 8388632
  88.9 34.3 %far_tiles.1.tiles_ref = bf16[16,128,3072]{2,1,0:T(8,128)(2,1)S(1)} custom-call(s32[640]{0:T(1024)S(1)} %reshape.23.idx_ref, bf16[256,8,128]{2,1,0:T(8,128)(2,1)S(1)} %all-to-all-done.2.got_ref, f32[16,3,128]{2,1,0:T(4,128)S(1)} %copy.62.pos_ref, f32[16,3,128]{2,1,0:T(4,128)S(1)} %copy.63.nrm_ref), custom_call_target="tpu_custom_call" | custom-call | flops 600000000 | tf_op jit(solution)/shard_map/far_tiles/pallas_call | solution.py:275
  123.2 4.5 %copy-done = bf16[16,128,3072]{2,1,0:T(8,128)(2,1)} copy-done((bf16[16,128,3072]{2,1,0:T(8,128)(2,1)}, bf16[16,128,3072]{2,1,0:T(8,128)(2,1)S(1)}, u32[]{:S(2)}) %copy-start) | copy-done | bytes 12582936
  127.7 4.6 %copy-done.1 = bf16[16,128,3072]{2,1,0:T(8,128)(2,1)S(1)} copy-done((bf16[16,128,3072]{2,1,0:T(8,128)(2,1)S(1)}, bf16[16,128,3072]{2,1,0:T(8,128)(2,1)}, u32[]{:S(2)}) %copy-start.1) | copy-done | bytes 12582936
  132.3 10.1 %far_bounce.2 = (bf16[16,75,128]{2,1,0:T(8,128)(2,1)S(1)}, f32[1,128]{1,0:T(1,128)S(1)}) custom-call(s32[640]{0:T(1024)S(1)} %reshape.23.idx_ref, bf16[256,80,128]{2,1,0:T(8,128)(2,1)} %all-to-all-done.1.got_ref, bf16[16,128,3072]{2,1,0:T(8,128)(2,1)S(1)} %copy-done.1, f32[16,75,128]{2,1,0:T(8,128)S(1)} %get-tuple-element.13.near_ref, ...), custom_call_target="tpu_custom_call" | custom-call | flops 500000000 | tf_op jit(solution)/shard_map/far_bounce/pallas_call | solution.py:317
  142.4 8.7 %pack_field.3 = bf16[256,80,128]{2,1,0:T(8,128)(2,1)S(1)} custom-call(s32[256]{0:T(256)S(1)} %reshape.24.req_ref, bf16[16,75,128]{2,1,0:T(8,128)(2,1)S(1)} %get-tuple-element.31.field_ref), custom_call_target="tpu_custom_call" | custom-call | flops 10000000 | tf_op jit(solution)/shard_map/pack_field/pallas_call | solution.py:135
  151.1 2.4 copy-done.4
  153.5 10.2 %all-to-all-start.3 = ((bf16[256,80,128]{2,1,0:T(8,128)(2,1)}), bf16[256,80,128]{2,1,0:T(8,128)(2,1)}, u32[]{:S(2)}, u32[]{:S(2)}) async-start(bf16[256,80,128]{2,1,0:T(8,128)(2,1)} %copy-done.4), calls=%async_computation.3 | async-start | bytes 10485760 | tf_op jit(solution)/shard_map/all_to_all | solution.py:343
  163.7 3.4 %copy-done.6 = bf16[16,128,2048]{2,1,0:T(8,128)(2,1)S(1)} copy-done((bf16[16,128,2048]{2,1,0:T(8,128)(2,1)S(1)}, bf16[16,128,2048]{2,1,0:T(8,128)(2,1)}, u32[]{:S(2)}) %copy-start.6) | copy-done | bytes 8388632
  167.0 5.8 %near_again.1.near_ref = f32[16,75,128]{2,1,0:T(8,128)S(1)} custom-call(s32[640]{0:T(1024)S(1)} %reshape.23.idx_ref, bf16[16,75,128]{2,1,0:T(8,128)(2,1)S(1)} %get-tuple-element.31.field_ref, bf16[16,128,2048]{2,1,0:T(8,128)(2,1)S(1)} %copy-done.6), custom_call_target="tpu_custom_call" | custom-call | flops 300000000 | tf_op jit(solution)/shard_map/near_again/pallas_call | solution.py:238
  172.8 53.2 %all-to-all-done.3.got_ref = bf16[256,80,128]{2,1,0:T(8,128)(2,1)} async-done(((bf16[256,80,128]{2,1,0:T(8,128)(2,1)}), bf16[256,80,128]{2,1,0:T(8,128)(2,1)}, u32[]{:S(2)}, u32[]{:S(2)}) %all-to-all-start.3) | async-done | bytes 5242912 | tf_op jit(solution)/shard_map/all_to_all | solution.py:343
  226.1 4.6 %copy-done.2 = bf16[16,128,3072]{2,1,0:T(8,128)(2,1)S(1)} copy-done((bf16[16,128,3072]{2,1,0:T(8,128)(2,1)S(1)}, bf16[16,128,3072]{2,1,0:T(8,128)(2,1)}, u32[]{:S(2)}) %copy-start.2) | copy-done | bytes 12582936
  230.7 10.1 %far_bounce.3 = (bf16[16,75,128]{2,1,0:T(8,128)(2,1)S(1)}, f32[1,128]{1,0:T(1,128)S(1)}) custom-call(s32[640]{0:T(1024)S(1)} %reshape.23.idx_ref, bf16[256,80,128]{2,1,0:T(8,128)(2,1)} %all-to-all-done.3.got_ref, bf16[16,128,3072]{2,1,0:T(8,128)(2,1)S(1)} %copy-done.2, f32[16,75,128]{2,1,0:T(8,128)S(1)} %near_again.1.near_ref, ...), custom_call_target="tpu_custom_call" | custom-call | flops 500000000 | tf_op jit(solution)/shard_map/far_bounce/pallas_call | solution.py:317
  241.5 5.5 %all-to-all-start.4 = ((f32[128,2,128]{2,1,0:T(2,128)}), f32[128,2,128]{2,1,0:T(2,128)S(1)}, u32[]{:S(2)}, u32[]{:S(2)}) async-start(f32[128,2,128]{2,1,0:T(2,128)} %broadcast_in_dim.2), calls=%async_computation.4 | async-start | bytes 262144 | tf_op jit(solution)/shard_map/all_to_all | solution.py:343
  247.0 0.8 copy.72
  247.8 0.8 copy.73
  248.6 8.6 %all-to-all-done.4 = f32[128,2,128]{2,1,0:T(2,128)S(1)} async-done(((f32[128,2,128]{2,1,0:T(2,128)}), f32[128,2,128]{2,1,0:T(2,128)S(1)}, u32[]{:S(2)}, u32[]{:S(2)}) %all-to-all-start.4) | async-done | bytes 131104 | tf_op jit(solution)/shard_map/all_to_all | solution.py:343
  (25 shorter events, 3.6 us)
Async XLA Ops:
  0.6 0.7 copy-start.9
  1.3 0.7 copy-start.10
  3.3 21.2 %all-to-all-start = ((s32[128,1,2]{2,1,0:T(1,128)}), s32[128,1,2]{2,1,0:T(1,128)S(1)}, u32[]{:S(2)}, u32[]{:S(2)}) async-start(s32[128,1,2]{2,1,0:T(1,128)} %bitcast.2), calls=%async_computation | async-start | bytes 131072 | tf_op jit(solution)/shard_map/all_to_all | solution.py:343
  26.0 0.7 copy-start.7
  28.5 18.4 %all-to-all-start.2 = ((bf16[256,8,128]{2,1,0:T(8,128)(2,1)}), bf16[256,8,128]{2,1,0:T(8,128)(2,1)S(1)}, u32[]{:S(2)}, u32[]{:S(2)}) async-start(bf16[256,8,128]{2,1,0:T(8,128)(2,1)} %pack_geometry.1), calls=%async_computation.2 | async-start | bytes 1048576 | tf_op jit(solution)/shard_map/all_to_all | solution.py:343
  42.6 2.4 copy-start.3
  44.9 10.2 %copy-start.11 = (f32[16,3,128]{2,0,1:T(8,128)S(1)}, f32[16,3,128]{2,0,1:T(8,128)}, u32[]{:S(2)}) copy-start(f32[16,3,128]{2,0,1:T(8,128)} %param.11) | copy-start | bytes 73732
  44.9 10.3 %copy-start.8 = (f32[16,128]{1,0:T(8,128)S(1)}, f32[16,128]{1,0:T(8,128)}, u32[]{:S(2)}) copy-start(f32[16,128]{1,0:T(8,128)} %param.10) | copy-start | bytes 24580
  47.0 80.7 %all-to-all-start.1 = ((bf16[256,80,128]{2,1,0:T(8,128)(2,1)}), bf16[256,80,128]{2,1,0:T(8,128)(2,1)}, u32[]{:S(2)}, u32[]{:S(2)}) async-start(bf16[256,80,128]{2,1,0:T(8,128)(2,1)} %copy-done.3), calls=%async_computation.1 | async-start | bytes 10485760 | tf_op jit(solution)/shard_map/all_to_all | solution.py:343
  85.7 3.2 %copy-start.5 = (bf16[16,128,2048]{2,1,0:T(8,128)(2,1)}, bf16[16,128,2048]{2,1,0:T(8,128)(2,1)S(1)}, u32[]{:S(2)}) copy-start(bf16[16,128,2048]{2,1,0:T(8,128)(2,1)S(1)} %get-tuple-element.15.tiles_ref) | copy-start | bytes 25165828
  123.1 4.5 %copy-start = (bf16[16,128,3072]{2,1,0:T(8,128)(2,1)}, bf16[16,128,3072]{2,1,0:T(8,128)(2,1)S(1)}, u32[]{:S(2)}) copy-start(bf16[16,128,3072]{2,1,0:T(8,128)(2,1)S(1)} %far_tiles.1.tiles_ref) | copy-start | bytes 37748740
  127.7 4.6 %copy-start.1 = (bf16[16,128,3072]{2,1,0:T(8,128)(2,1)S(1)}, bf16[16,128,3072]{2,1,0:T(8,128)(2,1)}, u32[]{:S(2)}) copy-start(bf16[16,128,3072]{2,1,0:T(8,128)(2,1)} %copy-done) | copy-start | bytes 37748740
  151.1 2.4 copy-start.4
  153.5 72.6 %all-to-all-start.3 = ((bf16[256,80,128]{2,1,0:T(8,128)(2,1)}), bf16[256,80,128]{2,1,0:T(8,128)(2,1)}, u32[]{:S(2)}, u32[]{:S(2)}) async-start(bf16[256,80,128]{2,1,0:T(8,128)(2,1)} %copy-done.4), calls=%async_computation.3 | async-start | bytes 10485760 | tf_op jit(solution)/shard_map/all_to_all | solution.py:343
  163.6 3.4 %copy-start.6 = (bf16[16,128,2048]{2,1,0:T(8,128)(2,1)S(1)}, bf16[16,128,2048]{2,1,0:T(8,128)(2,1)}, u32[]{:S(2)}) copy-start(bf16[16,128,2048]{2,1,0:T(8,128)(2,1)} %copy-done.5) | copy-start | bytes 25165828
  226.1 4.6 %copy-start.2 = (bf16[16,128,3072]{2,1,0:T(8,128)(2,1)S(1)}, bf16[16,128,3072]{2,1,0:T(8,128)(2,1)}, u32[]{:S(2)}) copy-start(bf16[16,128,3072]{2,1,0:T(8,128)(2,1)} %copy-done) | copy-start | bytes 37748740
  241.5 15.7 %all-to-all-start.4 = ((f32[128,2,128]{2,1,0:T(2,128)}), f32[128,2,128]{2,1,0:T(2,128)S(1)}, u32[]{:S(2)}, u32[]{:S(2)}) async-start(f32[128,2,128]{2,1,0:T(2,128)} %broadcast_in_dim.2), calls=%async_computation.4 | async-start | bytes 262144 | tf_op jit(solution)/shard_map/all_to_all | solution.py:343
where the time goes:
time: 259 us; the launch traced here: 258 us
  Pallas kernels  111 us (43%)
  waiting for transfers between devices  72.1 us (28%)
  starting transfers between devices  39.6 us (15%)
  local copies, waits for them, and re-layouts  32.7 us (13%)
    all_to_all x5, waiting for transfers between devices, swap(): return lax.all_to_all(value, AXES, split_axis=0, concat_axis=0, tiled=True)  72.1 us
    all_to_all x5, starting transfers between devices, swap(): return lax.all_to_all(value, AXES, split_axis=0, concat_axis=0, tiled=True)  39.6 us
    pallas_call x1, Pallas kernels, far_tiles(): pl.pallas_call(far_tiles_kernel, grid_spec=pltpu.PrefetchScalarGridSpec(n...  34.3 us
    unnamed x30, local copies, waits for them, and re-layouts  31.2 us
    pallas_call x1, Pallas kernels, near_first(): pl.pallas_call(near_kernel, grid_spec=pltpu.PrefetchScalarGridSpec(num_sc...  30.4 us
    pallas_call x2, Pallas kernels, far_bounce(): pl.pallas_call(far_kernel, grid_spec=pltpu.PrefetchScalarGridSpec(num_sca...  20.2 us
    pallas_call x2, Pallas kernels, pack_field(): pl.pallas_call(send_kernel, grid_spec=pltpu.PrefetchScalarGridSpec(num_sc...  17.4 us
    pallas_call x1, Pallas kernels, near_again(): pl.pallas_call(near_again_kernel, grid_spec=pltpu.PrefetchScalarGridSpec(...  5.81 us
  transfers between devices with their start and end apart: 5, of which 4 were waited for; matrix products, arithmetic and copies ran while one was open for 2% of the time, Pallas kernels for 31%

commit v1 on v0

v1 whole, which is shorter than its diff:
```python
import functools
import math

import jax
import jax.numpy as jnp
from jax import lax
from jax.experimental import pallas as pl
from jax.experimental.pallas import tpu as pltpu
from jax.sharding import Mesh
from jax.sharding import PartitionSpec as P

COLORS = 3
NEAR = 16
FAR = 24
PAIRS = NEAR + FAR
CAP = 2
CH = 75
CHP = 80
BLK = 16
VERT = 128
DEVS = 128
ROWS = DEVS * CAP
AXES = ("gx_0", "gx_1", "gy_0", "gy_1")

F32 = jnp.float32
BF16 = jnp.bfloat16
I32 = jnp.int32


def params(limit_mib=40):
    return pltpu.CompilerParams(
        dimension_semantics=("arbitrary",), vmem_limit_bytes=limit_mib * 1024 * 1024
    )


def cost(flops, read=0):
    return pl.CostEstimate(flops=int(flops), bytes_accessed=int(read), transcendentals=0)


def index_kernel(pairs_ref, home_ref, idx_ref, req_ref):
    home = home_ref[...]
    both = jnp.concatenate([home >> 4, home & 15], axis=0).astype(F32).astype(BF16)
    pairs = pairs_ref[...]
    low = pairs & 127
    high = pairs >> 7
    sub = lax.broadcasted_iota(I32, (VERT, PAIRS), 0)
    sub_f = sub.astype(F32)
    sub16 = lax.broadcasted_iota(I32, (16, PAIRS), 0)
    lane = lax.broadcasted_iota(I32, (VERT, PAIRS), 1)
    lane_row = lax.broadcasted_iota(I32, (1, PAIRS), 1)
    is_far = lane >= NEAR
    owners, locals_ = [], []
    least = jnp.full((VERT, PAIRS), 99.0, F32)
    most = jnp.full((VERT, PAIRS), -1.0, F32)
    for s in range(BLK):
        hot = jnp.where(sub == low[s : s + 1, :], 1.0, 0.0).astype(BF16)
        got = jnp.dot(both, hot, preferred_element_type=F32)
        here = sub16 == high[s : s + 1, :]
        owner = jnp.sum(jnp.where(here, got[:16], 0.0), axis=0, keepdims=True)
        local = jnp.sum(jnp.where(here, got[16:], 0.0), axis=0, keepdims=True)
        owners.append(owner)
        locals_.append(local)
        same = (sub_f == owner) & is_far
        least = jnp.minimum(least, jnp.where(same, local, 99.0))
        most = jnp.maximum(most, jnp.where(same, local, -1.0))
    lo = jnp.min(least, axis=1, keepdims=True)
    hi = jnp.max(most, axis=1, keepdims=True)
    for s in range(BLK):
        first = jnp.sum(jnp.where(sub_f == owners[s], lo, 0.0), axis=0, keepdims=True)
        far_row = owners[s] * 2.0 + jnp.where(locals_[s] == first, 0.0, 1.0)
        idx_ref[s : s + 1, :] = jnp.where(lane_row < NEAR, locals_[s], far_row).astype(I32)
    used = hi >= 0.0
    req_ref[:, 0:1] = jnp.where(used, lo, 0.0).astype(I32)
    req_ref[:, 1:2] = jnp.where(used, hi, 0.0).astype(I32)


def find_indices(pairs, home):
    return pl.pallas_call(
        index_kernel,
        out_shape=(
            jax.ShapeDtypeStruct((BLK, PAIRS), I32),
            jax.ShapeDtypeStruct((DEVS, CAP), I32),
        ),
        cost_estimate=cost(4e6),
        compiler_params=pltpu.CompilerParams(vmem_limit_bytes=8 * 1024 * 1024),
        name="indices",
    )(pairs, home.reshape(BLK, VERT))


def whole(*shape):
    return pl.BlockSpec(shape, lambda i, *_: (0,) * len(shape))


def slot(*shape):
    return pl.BlockSpec((1,) + shape, lambda i, *_: (i,) + (0,) * len(shape))


def in_hbm(value):
    return pltpu.with_memory_space_constraint(value, pltpu.HBM)


def grid_spec(prefetch, steps, in_specs, out_specs, scratch):
    return pltpu.PrefetchScalarGridSpec(
        num_scalar_prefetch=prefetch,
        grid=(steps,),
        in_specs=in_specs,
        out_specs=out_specs,
        scratch_shapes=scratch,
    )


def geometry_kernel(req_ref, pos_ref, nrm_ref, area_ref, out_ref, table):
    table[:, 0:3, :] = pos_ref[...]
    table[:, 3:6, :] = nrm_ref[...] * (area_ref[...] * (-1.0 / math.pi))
    table[:, 6:8, :] = jnp.ones((BLK, 2, VERT), F32)

    def put(i, carry):
        out_ref[i] = table[req_ref[i]].astype(BF16)
        return carry

    lax.fori_loop(0, ROWS, put, 0, unroll=8)


def pack_geometry(req, pos, nrm, area):
    return pl.pallas_call(
        geometry_kernel,
        grid_spec=grid_spec(
            1,
            1,
            [whole(BLK, 3, VERT), whole(BLK, 3, VERT), whole(BLK, 1, VERT)],
            whole(ROWS, 8, VERT),
            [pltpu.VMEM((BLK, 8, VERT), F32)],
        ),
        out_shape=jax.ShapeDtypeStruct((ROWS, 8, VERT), BF16),
        cost_estimate=cost(2e6),
        compiler_params=params(8),
        name="pack_geometry",
    )(req, pos, nrm, area)


PACK = 32


def send_kernel(req_ref, field_ref, out_ref, slab):
    step = pl.program_id(0)

    @pl.when(step == 0)
    def _():
        slab[:, 64:, :] = jnp.zeros((BLK, CHP - 64, VERT), BF16)
        slab[:, :CH, :] = field_ref[...]

    def put(i, carry):
        out_ref[i] = slab[req_ref[step * PACK + i]]
        return carry

    lax.fori_loop(0, PACK, put, 0, unroll=4)


def pack_field(req, field):
    return pl.pallas_call(
        send_kernel,
        grid_spec=grid_spec(
            1,
            ROWS // PACK,
            [whole(BLK, CH, VERT)],
            pl.BlockSpec((PACK, CHP, VERT), lambda i, *_: (i, 0, 0)),
            [pltpu.VMEM((BLK, CHP, VERT), BF16)],
        ),
        out_shape=pltpu.HBM((ROWS, CHP, VERT), BF16),
        cost_estimate=cost(1e7),
        compiler_params=params(8),
        name="pack_field",
    )(req, field)


def thirds(value):
    high = value.astype(BF16).astype(F32)
    rest = value - high
    middle = rest.astype(BF16).astype(F32)
    return high, middle, (rest - middle).astype(BF16).astype(F32)


NEAR_TERMS = ((0, 0), (0, 1), (1, 0), (1, 1), (0, 2), (2, 0))
FAR_TERMS = ((0, 0), (0, 1), (0, 2))


def stack_rows(parts):
    return jnp.concatenate(parts, axis=0)


def source_rows(geo, terms):
    parts = thirds(geo) if len(terms) > 3 else (geo,)
    square = geo[0:1] * geo[0:1] + geo[1:2] * geo[1:2] + geo[2:3] * geo[2:3] + 1.0
    facing = geo[3:4] * geo[0:1] + geo[4:5] * geo[1:2] + geo[5:6] * geo[2:3]
    zero = jnp.zeros((1, VERT), F32)
    alone = stack_rows([*thirds(square), *thirds(facing), zero, zero])
    return stack_rows([*[parts[i] for i, _ in terms], alone]).T.astype(BF16)


def receiver_rows(pos, nrm, terms):
    zero = jnp.zeros((1, VERT), F32)
    zeros3 = jnp.zeros((3, VERT), F32)
    one = jnp.ones((1, VERT), F32)
    square = pos[0:1] * pos[0:1] + pos[1:2] * pos[1:2] + pos[2:3] * pos[2:3]
    facing = nrm[0:1] * pos[0:1] + nrm[1:2] * pos[1:2] + nrm[2:3] * pos[2:3]
    forms = (
        (stack_rows([-2.0 * pos, zeros3, square, zero]), (1.0, 0.0)),
        (stack_rows([nrm, zeros3, -facing, zero]), (0.0, 0.0)),
        (stack_rows([zeros3, -pos, zero, zero]), (0.0, 1.0)),
    )
    out = []
    for rows, (with_square, with_facing) in forms:
        parts = thirds(rows)
        alone = stack_rows([one * with_square] * 3 + [one * with_facing] * 3 + [zero, zero])
        out.append(stack_rows([*[parts[j] for _, j in terms], alone]))
    return jnp.concatenate(out, axis=1).astype(BF16)


def fill_tiles(index_of, count, recv, table, out_ref):
    right = recv[...]
    for j in range(count):
        got = jnp.dot(table[index_of(j)], right, preferred_element_type=F32)
        soft = got[:, :VERT]
        value = jnp.maximum(got[:, VERT : 2 * VERT], 0.0) * jnp.maximum(got[:, 2 * VERT :], 0.0)
        value = value / (soft * soft)
        out_ref[0, j * VERT : (j + 1) * VERT, :] = value.astype(BF16)


def product(left, right):
    return jnp.dot(left, right, preferred_element_type=F32)


def near_kernel(idx_ref, field_ref, pos_ref, nrm_ref, area_ref, tiles_ref, sum_ref, table, recv, rows):
    s = pl.program_id(0)

    @pl.when(s == 0)
    def _():
        def make(t, carry):
            scaled = nrm_ref[t] * (area_ref[t] * (-1.0 / math.pi))
            geo = stack_rows([pos_ref[t], scaled, jnp.ones((2, VERT), F32)])
            table[t] = source_rows(geo, NEAR_TERMS)
            return carry

        lax.fori_loop(0, BLK, make, 0)

    recv[...] = receiver_rows(pos_ref[s], nrm_ref[s], NEAR_TERMS)
    fill_tiles(lambda j: idx_ref[s * PAIRS + j], NEAR, recv, table, tiles_ref)
    for j in range(NEAR):
        rows[:, j * VERT : (j + 1) * VERT] = field_ref[idx_ref[s * PAIRS + j]]
    sum_ref[0] = product(rows[...], tiles_ref[0])


NEAR_K = 8 * (len(NEAR_TERMS) + 1)
FAR_K = 8 * (len(FAR_TERMS) + 1)


def near_first(idx, field, pos, nrm, area):
    return pl.pallas_call(
        near_kernel,
        grid_spec=grid_spec(
            1,
            BLK,
            [whole(BLK, CH, VERT), whole(BLK, 3, VERT), whole(BLK, 3, VERT), whole(BLK, 1, VERT)],
            [slot(NEAR * VERT, VERT), slot(CH, VERT)],
            [
                pltpu.VMEM((BLK, VERT, NEAR_K), BF16),
                pltpu.VMEM((NEAR_K, 3 * VERT), BF16),
                pltpu.VMEM((CH, NEAR * VERT), BF16),
            ],
        ),
        out_shape=(
            pltpu.HBM((BLK, NEAR * VERT, VERT), BF16),
            jax.ShapeDtypeStruct((BLK, CH, VERT), F32),
        ),
        cost_estimate=cost(6e8),
        compiler_params=params(),
        name="near_first",
    )(idx, field, pos, nrm, area)


def near_again_kernel(idx_ref, field_ref, tiles_ref, sum_ref, rows, tiles, sems):
    s = pl.program_id(0)

    def copies(at):
        return pltpu.make_async_copy(tiles_ref.at[at], tiles.at[at], sems.at[at])

    @pl.when(s == 0)
    def _():
        for at in range(BLK):
            copies(at).start()

    copies(s).wait()
    for j in range(NEAR):
        rows[:, j * VERT : (j + 1) * VERT] = field_ref[idx_ref[s * PAIRS + j]]
    sum_ref[0] = product(rows[...], tiles[s])


def near_again(idx, field, tiles):
    return pl.pallas_call(
        near_again_kernel,
        grid_spec=grid_spec(
            1,
            BLK,
            [whole(BLK, CH, VERT), pl.BlockSpec(memory_space=pltpu.HBM)],
            slot(CH, VERT),
            [
                pltpu.VMEM((CH, NEAR * VERT), BF16),
                pltpu.VMEM((BLK, NEAR * VERT, VERT), BF16),
                pltpu.SemaphoreType.DMA((BLK,)),
            ],
        ),
        out_shape=jax.ShapeDtypeStruct((BLK, CH, VERT), F32),
        cost_estimate=cost(3e8),
        compiler_params=params(),
        name="near_again",
    )(idx, field, in_hbm(tiles))


def far_tiles_kernel(idx_ref, got_ref, pos_ref, nrm_ref, tiles_ref, table, recv):
    s = pl.program_id(0)

    @pl.when(s == 0)
    def _():
        def make(t, carry):
            table[t] = source_rows(got_ref[t].astype(F32), FAR_TERMS)
            return carry

        lax.fori_loop(0, ROWS, make, 0, unroll=4)

    recv[...] = receiver_rows(pos_ref[s], nrm_ref[s], FAR_TERMS)
    fill_tiles(lambda j: idx_ref[s * PAIRS + NEAR + j], FAR, recv, table, tiles_ref)


def far_tiles(idx, got, pos, nrm):
    return pl.pallas_call(
        far_tiles_kernel,
        grid_spec=grid_spec(
            1,
            BLK,
            [whole(ROWS, 8, VERT), whole(BLK, 3, VERT), whole(BLK, 3, VERT)],
            slot(FAR * VERT, VERT),
            [pltpu.VMEM((ROWS, VERT, FAR_K), BF16), pltpu.VMEM((FAR_K, 3 * VERT), BF16)],
        ),
        out_shape=pltpu.HBM((BLK, FAR * VERT, VERT), BF16),
        cost_estimate=cost(6e8),
        compiler_params=params(),
        name="far_tiles",
    )(idx, got, pos, nrm)


def far_kernel(
    idx_ref, got_ref, tiles_ref, near_ref, albedo_ref, area_ref, out_ref, energy_ref, rows, field, tiles, sems
):
    s = pl.program_id(0)

    def copies(at):
        return pltpu.make_async_copy(tiles_ref.at[at], tiles.at[at], sems.at[at])

    @pl.when(s == 0)
    def _():
        whole_field = pltpu.make_async_copy(got_ref, field, sems.at[BLK])
        whole_field.start()
        for at in range(BLK):
            copies(at).start()
        whole_field.wait()

    copies(s).wait()
    for j in range(FAR):
        rows[:, j * VERT : (j + 1) * VERT] = field[idx_ref[s * PAIRS + NEAR + j]]
    total = near_ref[0] + product(rows[...], tiles[s])[:CH]
    channel = lax.broadcasted_iota(I32, (CH, VERT), 0)
    shade = jnp.where(
        channel < CH // COLORS,
        albedo_ref[0, 0:1, :],
        jnp.where(channel < 2 * (CH // COLORS), albedo_ref[0, 1:2, :], albedo_ref[0, 2:3, :]),
    )
    bounce = total * shade
    out_ref[0] = bounce.astype(BF16)
    share = jnp.sum(area_ref[0] * bounce * bounce, axis=0, keepdims=True)

    @pl.when(s == 0)
    def _():
        energy_ref[...] = share

    @pl.when(s > 0)
    def _():
        energy_ref[...] = energy_ref[...] + share


def far_bounce(idx, got, tiles, near, albedo, area):
    return pl.pallas_call(
        far_kernel,
        grid_spec=grid_spec(
            1,
            BLK,
            [
                pl.BlockSpec(memory_space=pltpu.HBM),
                pl.BlockSpec(memory_space=pltpu.HBM),
                slot(CH, VERT),
                slot(COLORS, VERT),
                slot(1, VERT),
            ],
            [slot(CH, VERT), whole(1, VERT)],
            [
                pltpu.VMEM((CHP, FAR * VERT), BF16),
                pltpu.VMEM((ROWS, CHP, VERT), BF16),
                pltpu.VMEM((BLK, FAR * VERT, VERT), BF16),
                pltpu.SemaphoreType.DMA((BLK + 1,)),
            ],
        ),
        out_shape=(
            jax.ShapeDtypeStruct((BLK, CH, VERT), BF16),
            jax.ShapeDtypeStruct((1, VERT), F32),
        ),
        cost_estimate=cost(5e8),
        compiler_params=params(),
        name="far_bounce",
    )(idx, got, in_hbm(tiles), near, albedo, area)


def swap(value):
    return lax.all_to_all(value, AXES, split_axis=0, concat_axis=0, tiled=True)


def body(transfer, positions, normals, area, albedo, pairs, home):
    area_row = area.reshape(BLK, 1, VERT)
    idx, need = find_indices(pairs, home)
    idx = idx.reshape(-1)
    asked = swap(need).reshape(-1)
    near_tiles, near_one = near_first(idx, transfer, positions, normals, area_row)
    geometry = swap(pack_geometry(asked, positions, normals, area_row))
    got_one = swap(pack_field(asked, transfer))
    tiles = far_tiles(idx, geometry, positions, normals)
    bounce_one, share_one = far_bounce(idx, got_one, tiles, near_one, albedo, area_row)
    got_two = swap(pack_field(asked, bounce_one))
    near_two = near_again(idx, bounce_one, near_tiles)
    bounce_two, share_two = far_bounce(idx, got_two, tiles, near_two, albedo, area_row)
    shares = jnp.concatenate([share_one, share_two], axis=0)
    shares = swap(jnp.broadcast_to(shares[None], (DEVS, 2, VERT)))
    energies = jnp.sum(shares, axis=(0, 2)) * (1.0 / (DEVS * BLK * VERT * CH))
    return bounce_one, bounce_two, energies


def solution(mesh):
    finer = Mesh(mesh.devices.reshape(4, 2, 4, 4), AXES)
    three = P(AXES, None, None)
    return jax.shard_map(
        body,
        mesh=finer,
        in_specs=(three, three, three, P(AXES, None), three, P(AXES, None), P()),
        out_specs=(three, three, P()),
        check_vma=False,
    )
```

time: 259 us -> 225 us (0.87)
  Pallas kernels: 111 us -> 75.8 us
  waiting for transfers between devices: 72.1 us -> 106 us
  local copies, waits for them, and re-layouts: 32.7 us -> 7.67 us
  starting transfers between devices: 39.6 us -> 32.2 us
    pallas_call x8, Pallas kernels: 110 us -> 74.5 us  [the longest x1 22.8 us: far_tiles(): pl.pallas_call(far_tiles_kernel, grid_spec=grid_spec(1, BLK, [whole(ROWS,...]
    all_to_all x5, waiting for transfers between devices: 72.1 us -> 106 us  [swap(): return lax.all_to_all(value, AXES, split_axis=0, concat_axis=0, tiled=True)]
    unnamed x30 -> x16, local copies, waits for them, and re-layouts: 31.2 us -> 6.26 us
    all_to_all x5, starting transfers between devices: 39.6 us -> 32.2 us  [swap(): return lax.all_to_all(value, AXES, split_axis=0, concat_axis=0, tiled=True)]
  transfers between devices with their start and end apart: 5 -> 5, of which waited for: 4 -> 5; matrix products, arithmetic and copies ran while one was open for 2% -> 2% of each run, Pallas kernels for 31% -> 22%
where the time goes in v1:
time: 225 us; the launch traced here: 224 us
  waiting for transfers between devices  106 us (47%)
  Pallas kernels  75.8 us (34%)
  starting transfers between devices  32.2 us (14%)
  local copies, waits for them, and re-layouts  7.67 us (3%)
    all_to_all x5, waiting for transfers between devices, swap(): return lax.all_to_all(value, AXES, split_axis=0, concat_axis=0, tiled=True)  106 us
    all_to_all x5, starting transfers between devices, swap(): return lax.all_to_all(value, AXES, split_axis=0, concat_axis=0, tiled=True)  32.2 us
    pallas_call x1, Pallas kernels, far_tiles(): pl.pallas_call(far_tiles_kernel, grid_spec=grid_spec(1, BLK, [whole(ROWS,...  22.8 us
    pallas_call x2, Pallas kernels, far_bounce(): pl.pallas_call(far_kernel, grid_spec=grid_spec(1, BLK, [pl.BlockSpec(memo...  19.2 us
    pallas_call x1, Pallas kernels, near_first(): pl.pallas_call(near_kernel, grid_spec=grid_spec(1, BLK, [whole(BLK, CH, V...  15 us
    pallas_call x2, Pallas kernels, pack_field(): pl.pallas_call(send_kernel, grid_spec=grid_spec(1, ROWS // PACK, [whole(B...  9.25 us
    pallas_call x1, Pallas kernels, near_again(): pl.pallas_call(near_again_kernel, grid_spec=grid_spec(1, BLK, [whole(BLK,...  6.43 us
    unnamed x16, local copies, waits for them, and re-layouts  6.26 us
  transfers between devices with their start and end apart: 5, of which 5 were waited for; matrix products, arithmetic and copies ran while one was open for 2% of the time, Pallas kernels for 22%

profile of v1, /device:TPU:1, one launch (start us, length us, event | category | flops | bytes accessed | tf_op | source)
XLA Modules:
  0.0 223.9 jit_solution(15571322626262183283)
XLA Ops:
  0.6 0.7 copy-done.2
  1.3 0.7 copy-done.3
  2.0 1.3 indices.1
  3.3 11.5 %all-to-all-start = ((s32[128,1,2]{2,1,0:T(1,128)}), s32[128,1,2]{2,1,0:T(1,128)S(1)}, u32[]{:S(2)}, u32[]{:S(2)}) async-start(s32[128,1,2]{2,1,0:T(1,128)} %bitcast.2), calls=%async_computation | async-start | bytes 131072 | tf_op jit(solution)/shard_map/all_to_all | solution.py:422
  14.8 0.8 copy.62.pos_ref
  15.6 0.8 copy.63.nrm_ref
  16.3 8.2 %all-to-all-done = s32[128,1,2]{2,1,0:T(1,128)S(1)} async-done(((s32[128,1,2]{2,1,0:T(1,128)}), s32[128,1,2]{2,1,0:T(1,128)S(1)}, u32[]{:S(2)}, u32[]{:S(2)}) %all-to-all-start) | async-done | bytes 1056 | tf_op jit(solution)/shard_map/all_to_all | solution.py:422
  24.6 0.5 broadcast.9
  25.1 0.8 reduce.3
  26.0 0.7 copy-done
  26.7 1.8 pack_geometry.1
  28.6 4.3 %all-to-all-start.2 = ((bf16[256,8,128]{2,1,0:T(8,128)(2,1)}), bf16[256,8,128]{2,1,0:T(8,128)(2,1)S(1)}, u32[]{:S(2)}, u32[]{:S(2)}) async-start(bf16[256,8,128]{2,1,0:T(8,128)(2,1)} %pack_geometry.1), calls=%async_computation.2 | async-start | bytes 1048576 | tf_op jit(solution)/shard_map/all_to_all | solution.py:422
  32.8 1.1 copy.61.field_ref
  33.9 4.6 %pack_field.2 = bf16[256,80,128]{2,1,0:T(8,128)(2,1)} custom-call(s32[256]{0:T(256)S(1)} %reshape.24.req_ref, bf16[16,75,128]{2,1,0:T(8,128)(2,1)S(1)} %copy.61.field_ref), custom_call_target="tpu_custom_call" | custom-call | flops 10000000 | tf_op jit(solution)/shard_map/pack_field/pallas_call | solution.py:160
  38.5 8.4 %all-to-all-done.2.got_ref = bf16[256,8,128]{2,1,0:T(8,128)(2,1)S(1)} async-done(((bf16[256,8,128]{2,1,0:T(8,128)(2,1)}), bf16[256,8,128]{2,1,0:T(8,128)(2,1)S(1)}, u32[]{:S(2)}, u32[]{:S(2)}) %all-to-all-start.2) | async-done | bytes 524320 | tf_op jit(solution)/shard_map/all_to_all | solution.py:422
  47.0 5.1 %all-to-all-start.1 = ((bf16[256,80,128]{2,1,0:T(8,128)(2,1)}), bf16[256,80,128]{2,1,0:T(8,128)(2,1)}, u32[]{:S(2)}, u32[]{:S(2)}) async-start(bf16[256,80,128]{2,1,0:T(8,128)(2,1)} %pack_field.2), calls=%async_computation.1 | async-start | bytes 10485760 | tf_op jit(solution)/shard_map/all_to_all | solution.py:422
  52.2 15.0 %near_first.1 = (bf16[16,2048,128]{2,1,0:T(8,128)(2,1)}, f32[16,75,128]{2,1,0:T(8,128)S(1)}) custom-call(s32[640]{0:T(1024)S(1)} %reshape.23.idx_ref, bf16[16,75,128]{2,1,0:T(8,128)(2,1)S(1)} %copy.61.field_ref, f32[16,3,128]{2,1,0:T(4,128)S(1)} %copy.62.pos_ref, f32[16,3,128]{2,1,0:T(4,128)S(1)} %copy.63.nrm_ref, f32[16,1,128]{2,1,0:T(1,128)S(1)} %bitcast.6), custom_call_target="tpu_custom_call" | custom-call | flops 600000000 | tf_op jit(solution)/shard_map/near_first/pallas_call | solution.py:258
  67.2 22.8 %far_tiles.1.tiles_ref = bf16[16,3072,128]{2,1,0:T(8,128)(2,1)} custom-call(s32[640]{0:T(1024)S(1)} %reshape.23.idx_ref, bf16[256,8,128]{2,1,0:T(8,128)(2,1)S(1)} %all-to-all-done.2.got_ref, f32[16,3,128]{2,1,0:T(4,128)S(1)} %copy.62.pos_ref, f32[16,3,128]{2,1,0:T(4,128)S(1)} %copy.63.nrm_ref), custom_call_target="tpu_custom_call" | custom-call | flops 600000000 | tf_op jit(solution)/shard_map/far_tiles/pallas_call | solution.py:335
  90.0 24.7 %all-to-all-done.1.got_ref = bf16[256,80,128]{2,1,0:T(8,128)(2,1)} async-done(((bf16[256,80,128]{2,1,0:T(8,128)(2,1)}), bf16[256,80,128]{2,1,0:T(8,128)(2,1)}, u32[]{:S(2)}, u32[]{:S(2)}) %all-to-all-start.1) | async-done | bytes 5242912 | tf_op jit(solution)/shard_map/all_to_all | solution.py:422
  114.6 9.6 %far_bounce.2 = (bf16[16,75,128]{2,1,0:T(8,128)(2,1)S(1)}, f32[1,128]{1,0:T(1,128)S(1)}) custom-call(s32[640]{0:T(1024)S(1)} %reshape.23.idx_ref, bf16[256,80,128]{2,1,0:T(8,128)(2,1)} %all-to-all-done.1.got_ref, bf16[16,3072,128]{2,1,0:T(8,128)(2,1)} %far_tiles.1.tiles_ref, f32[16,75,128]{2,1,0:T(8,128)S(1)} %get-tuple-element.13.near_ref, ...), custom_call_target="tpu_custom_call" | custom-call | flops 500000000 | tf_op jit(solution)/shard_map/far_bounce/pallas_call | solution.py:391
  124.2 4.6 %pack_field.3 = bf16[256,80,128]{2,1,0:T(8,128)(2,1)} custom-call(s32[256]{0:T(256)S(1)} %reshape.24.req_ref, bf16[16,75,128]{2,1,0:T(8,128)(2,1)S(1)} %get-tuple-element.31.field_ref), custom_call_target="tpu_custom_call" | custom-call | flops 10000000 | tf_op jit(solution)/shard_map/pack_field/pallas_call | solution.py:160
  128.8 5.9 %all-to-all-start.3 = ((bf16[256,80,128]{2,1,0:T(8,128)(2,1)}), bf16[256,80,128]{2,1,0:T(8,128)(2,1)}, u32[]{:S(2)}, u32[]{:S(2)}) async-start(bf16[256,80,128]{2,1,0:T(8,128)(2,1)} %pack_field.3), calls=%async_computation.3 | async-start | bytes 10485760 | tf_op jit(solution)/shard_map/all_to_all | solution.py:422
  134.7 6.4 %near_again.1.near_ref = f32[16,75,128]{2,1,0:T(8,128)S(1)} custom-call(s32[640]{0:T(1024)S(1)} %reshape.23.idx_ref, bf16[16,75,128]{2,1,0:T(8,128)(2,1)S(1)} %get-tuple-element.31.field_ref, bf16[16,2048,128]{2,1,0:T(8,128)(2,1)} %get-tuple-element.15.tiles_ref), custom_call_target="tpu_custom_call" | custom-call | flops 300000000 | tf_op jit(solution)/shard_map/near_again/pallas_call | solution.py:299
  141.2 56.0 %all-to-all-done.3.got_ref = bf16[256,80,128]{2,1,0:T(8,128)(2,1)} async-done(((bf16[256,80,128]{2,1,0:T(8,128)(2,1)}), bf16[256,80,128]{2,1,0:T(8,128)(2,1)}, u32[]{:S(2)}, u32[]{:S(2)}) %all-to-all-start.3) | async-done | bytes 5242912 | tf_op jit(solution)/shard_map/all_to_all | solution.py:422
  197.2 9.6 %far_bounce.3 = (bf16[16,75,128]{2,1,0:T(8,128)(2,1)S(1)}, f32[1,128]{1,0:T(1,128)S(1)}) custom-call(s32[640]{0:T(1024)S(1)} %reshape.23.idx_ref, bf16[256,80,128]{2,1,0:T(8,128)(2,1)} %all-to-all-done.3.got_ref, bf16[16,3072,128]{2,1,0:T(8,128)(2,1)} %far_tiles.1.tiles_ref, f32[16,75,128]{2,1,0:T(8,128)S(1)} %near_again.1.near_ref, ...), custom_call_target="tpu_custom_call" | custom-call | flops 500000000 | tf_op jit(solution)/shard_map/far_bounce/pallas_call | solution.py:391
  206.8 0.7 broadcast_in_dim.2
  207.5 5.5 %all-to-all-start.4 = ((f32[128,2,128]{2,1,0:T(2,128)}), f32[128,2,128]{2,1,0:T(2,128)S(1)}, u32[]{:S(2)}, u32[]{:S(2)}) async-start(f32[128,2,128]{2,1,0:T(2,128)} %broadcast_in_dim.2), calls=%async_computation.4 | async-start | bytes 262144 | tf_op jit(solution)/shard_map/all_to_all | solution.py:422
  213.0 0.8 copy.72
  213.8 0.8 copy.73
  214.6 8.6 %all-to-all-done.4 = f32[128,2,128]{2,1,0:T(2,128)S(1)} async-done(((f32[128,2,128]{2,1,0:T(2,128)}), f32[128,2,128]{2,1,0:T(2,128)S(1)}, u32[]{:S(2)}, u32[]{:S(2)}) %all-to-all-start.4) | async-done | bytes 131104 | tf_op jit(solution)/shard_map/all_to_all | solution.py:422
  223.2 0.3 reduce_sum.9
  223.4 0.5 broadcast_multiply_fusion
  (11 shorter events, 0.3 us)
Async XLA Ops:
  0.6 0.7 copy-start.2
  1.3 0.7 copy-start.3
  3.3 21.2 %all-to-all-start = ((s32[128,1,2]{2,1,0:T(1,128)}), s32[128,1,2]{2,1,0:T(1,128)S(1)}, u32[]{:S(2)}, u32[]{:S(2)}) async-start(s32[128,1,2]{2,1,0:T(1,128)} %bitcast.2), calls=%async_computation | async-start | bytes 131072 | tf_op jit(solution)/shard_map/all_to_all | solution.py:422
  26.0 0.7 copy-start
  28.6 18.4 %all-to-all-start.2 = ((bf16[256,8,128]{2,1,0:T(8,128)(2,1)}), bf16[256,8,128]{2,1,0:T(8,128)(2,1)S(1)}, u32[]{:S(2)}, u32[]{:S(2)}) async-start(bf16[256,8,128]{2,1,0:T(8,128)(2,1)} %pack_geometry.1), calls=%async_computation.2 | async-start | bytes 1048576 | tf_op jit(solution)/shard_map/all_to_all | solution.py:422
  38.5 13.5 %copy-start.4 = (f32[16,3,128]{2,0,1:T(8,128)S(1)}, f32[16,3,128]{2,0,1:T(8,128)}, u32[]{:S(2)}) copy-start(f32[16,3,128]{2,0,1:T(8,128)} %param.11) | copy-start | bytes 73732
  38.5 13.6 %copy-start.1 = (f32[16,128]{1,0:T(8,128)S(1)}, f32[16,128]{1,0:T(8,128)}, u32[]{:S(2)}) copy-start(f32[16,128]{1,0:T(8,128)} %param.10) | copy-start | bytes 24580
  47.0 67.7 %all-to-all-start.1 = ((bf16[256,80,128]{2,1,0:T(8,128)(2,1)}), bf16[256,80,128]{2,1,0:T(8,128)(2,1)}, u32[]{:S(2)}, u32[]{:S(2)}) async-start(bf16[256,80,128]{2,1,0:T(8,128)(2,1)} %pack_field.2), calls=%async_computation.1 | async-start | bytes 10485760 | tf_op jit(solution)/shard_map/all_to_all | solution.py:422
  128.8 68.3 %all-to-all-start.3 = ((bf16[256,80,128]{2,1,0:T(8,128)(2,1)}), bf16[256,80,128]{2,1,0:T(8,128)(2,1)}, u32[]{:S(2)}, u32[]{:S(2)}) async-start(bf16[256,80,128]{2,1,0:T(8,128)(2,1)} %pack_field.3), calls=%async_computation.3 | async-start | bytes 10485760 | tf_op jit(solution)/shard_map/all_to_all | solution.py:422
  207.5 15.7 %all-to-all-start.4 = ((f32[128,2,128]{2,1,0:T(2,128)}), f32[128,2,128]{2,1,0:T(2,128)S(1)}, u32[]{:S(2)}, u32[]{:S(2)}) async-start(f32[128,2,128]{2,1,0:T(2,128)} %broadcast_in_dim.2), calls=%async_computation.4 | async-start | bytes 262144 | tf_op jit(solution)/shard_map/all_to_all | solution.py:422

commit v2 on v1

--- a/solution.py
+++ b/solution.py
@@ -15,7 +15,10 @@
 PAIRS = NEAR + FAR
 CAP = 2
 CH = 75
-CHP = 80
+MAIN = 64
+REST = CH - MAIN
+SECOND = 12
+WIRE = 2 * MAIN + 24
 BLK = 16
 VERT = 128
 DEVS = 128
@@ -27,6 +30,10 @@
 I32 = jnp.int32
 
 
+def in_hbm(value):
+    return pltpu.with_memory_space_constraint(value, pltpu.HBM)
+
+
 def params(limit_mib=40):
     return pltpu.CompilerParams(
         dimension_semantics=("arbitrary",), vmem_limit_bytes=limit_mib * 1024 * 1024
@@ -37,7 +44,13 @@
     return pl.CostEstimate(flops=int(flops), bytes_accessed=int(read), transcendentals=0)
 
 
-def index_kernel(pairs_ref, home_ref, idx_ref, req_ref):
+def index_kernel(pairs_hbm, home_hbm, idx_ref, req_ref, pairs_ref, home_ref, sems):
+    first = pltpu.make_async_copy(pairs_hbm, pairs_ref, sems.at[0])
+    second = pltpu.make_async_copy(home_hbm, home_ref, sems.at[1])
+    first.start()
+    second.start()
+    first.wait()
+    second.wait()
     home = home_ref[...]
     both = jnp.concatenate([home >> 4, home & 15], axis=0).astype(F32).astype(BF16)
     pairs = pairs_ref[...]
@@ -81,10 +94,16 @@
             jax.ShapeDtypeStruct((BLK, PAIRS), I32),
             jax.ShapeDtypeStruct((DEVS, CAP), I32),
         ),
+        in_specs=[pl.BlockSpec(memory_space=pltpu.HBM), pl.BlockSpec(memory_space=pltpu.HBM)],
+        scratch_shapes=[
+            pltpu.VMEM((BLK, PAIRS), I32),
+            pltpu.VMEM((BLK, VERT), I32),
+            pltpu.SemaphoreType.DMA((2,)),
+        ],
         cost_estimate=cost(4e6),
         compiler_params=pltpu.CompilerParams(vmem_limit_bytes=8 * 1024 * 1024),
         name="indices",
-    )(pairs, home.reshape(BLK, VERT))
+    )(in_hbm(pairs), in_hbm(home.reshape(BLK, VERT)))
 
 
 def whole(*shape):
@@ -93,10 +112,6 @@
 
 def slot(*shape):
     return pl.BlockSpec((1,) + shape, lambda i, *_: (i,) + (0,) * len(shape))
-
-
-def in_hbm(value):
-    return pltpu.with_memory_space_constraint(value, pltpu.HBM)
 
 
 def grid_spec(prefetch, steps, in_specs, out_specs, scratch):
@@ -109,11 +124,23 @@
     )
 
 
-def geometry_kernel(req_ref, pos_ref, nrm_ref, area_ref, out_ref, table):
-    table[:, 0:3, :] = pos_ref[...]
-    table[:, 3:6, :] = nrm_ref[...] * (area_ref[...] * (-1.0 / math.pi))
-    table[:, 6:8, :] = jnp.ones((BLK, 2, VERT), F32)
-
+def table_kernel(pos_ref, nrm_ref, area_ref, out_ref):
+    out_ref[:, 0:3, :] = pos_ref[...]
+    out_ref[:, 3:6, :] = nrm_ref[...] * (area_ref[...] * (-1.0 / math.pi))
+    out_ref[:, 6:8, :] = jnp.ones((BLK, 2, VERT), F32)
+
+
+def source_table(pos, nrm, area):
+    return pl.pallas_call(
+        table_kernel,
+        out_shape=jax.ShapeDtypeStruct((BLK, 8, VERT), F32),
+        cost_estimate=cost(1e6),
+        compiler_params=pltpu.CompilerParams(vmem_limit_bytes=8 * 1024 * 1024),
+        name="source_table",
+    )(pos, nrm, area)
+
+
+def geometry_kernel(req_ref, table, out_ref):
     def put(i, carry):
         out_ref[i] = table[req_ref[i]].astype(BF16)
         return carry
@@ -121,39 +148,113 @@
     lax.fori_loop(0, ROWS, put, 0, unroll=8)
 
 
-def pack_geometry(req, pos, nrm, area):
+def pack_geometry(req, table):
     return pl.pallas_call(
         geometry_kernel,
-        grid_spec=grid_spec(
-            1,
-            1,
-            [whole(BLK, 3, VERT), whole(BLK, 3, VERT), whole(BLK, 1, VERT)],
-            whole(ROWS, 8, VERT),
-            [pltpu.VMEM((BLK, 8, VERT), F32)],
-        ),
+        grid_spec=grid_spec(1, 1, [whole(BLK, 8, VERT)], whole(ROWS, 8, VERT), []),
         out_shape=jax.ShapeDtypeStruct((ROWS, 8, VERT), BF16),
         cost_estimate=cost(2e6),
         compiler_params=params(8),
         name="pack_geometry",
-    )(req, pos, nrm, area)
-
-
-PACK = 32
-
-
-def send_kernel(req_ref, field_ref, out_ref, slab):
-    step = pl.program_id(0)
-
-    @pl.when(step == 0)
-    def _():
-        slab[:, 64:, :] = jnp.zeros((BLK, CHP - 64, VERT), BF16)
-        slab[:, :CH, :] = field_ref[...]
-
-    def put(i, carry):
-        out_ref[i] = slab[req_ref[step * PACK + i]]
+    )(req, table)
+
+
+def invert_kernel(req_ref, order_ref, start_ref, at):
+    def clear(b, carry):
+        start_ref[b] = 0
         return carry
 
-    lax.fori_loop(0, PACK, put, 0, unroll=4)
+    lax.fori_loop(0, BLK + 1, clear, 0)
+
+    def count(i, carry):
+        b = req_ref[i] + 1
+        start_ref[b] = start_ref[b] + 1
+        return carry
+
+    lax.fori_loop(0, ROWS, count, 0)
+
+    def add(b, total):
+        at[b] = total
+        total = total + start_ref[b + 1]
+        start_ref[b + 1] = total
+        return total
+
+    lax.fori_loop(0, BLK, add, 0)
+
+    def place(i, carry):
+        b = req_ref[i]
+        order_ref[at[b]] = i
+        at[b] = at[b] + 1
+        return carry
+
+    lax.fori_loop(0, ROWS, place, 0)
+
+
+def invert(req):
+    smem = pl.BlockSpec(memory_space=pltpu.SMEM)
+    return pl.pallas_call(
+        invert_kernel,
+        grid_spec=grid_spec(1, 1, [], [smem, smem], [pltpu.SMEM((BLK,), I32)]),
+        out_shape=(
+            jax.ShapeDtypeStruct((ROWS,), I32),
+            jax.ShapeDtypeStruct((BLK + 1,), I32),
+        ),
+        cost_estimate=cost(1e7),
+        compiler_params=params(8),
+        name="invert",
+    )(req)
+
+
+def ends(last):
+    last = last.astype(F32)
+    zeros = lambda n: jnp.zeros((n, VERT), F32)
+    low = jnp.concatenate([last, zeros(32 - REST)], axis=0)
+    high = jnp.concatenate([zeros(SECOND), last, zeros(32 - SECOND - REST)], axis=0)
+    return low.astype(BF16), high.astype(BF16)
+
+
+def send_main(slab, b, i, out_ref, sem):
+    at = pl.multiple_of((i & 1) * MAIN, MAIN)
+    pltpu.make_async_copy(
+        slab.at[b, pl.ds(0, MAIN)], out_ref.at[i >> 1, pl.ds(at, MAIN)], sem
+    ).start()
+
+
+def send_ends(req_ref, low, high, both, out_ref, sems):
+    def put(d, carry):
+        both[d] = low[req_ref[2 * d]] + high[req_ref[2 * d + 1]]
+        return carry
+
+    lax.fori_loop(0, DEVS, put, 0, unroll=8)
+    tail = pltpu.make_async_copy(
+        both.at[:, pl.ds(0, 24)], out_ref.at[:, pl.ds(2 * MAIN, 24)], sems.at[1]
+    )
+    tail.start()
+    main = out_ref.at[:, pl.ds(0, 2 * MAIN)]
+    pltpu.make_async_copy(main, main, sems.at[0]).wait()
+    tail.wait()
+
+
+SEND_SCRATCH = [
+    pltpu.VMEM((BLK, 32, VERT), BF16),
+    pltpu.VMEM((BLK, 32, VERT), BF16),
+    pltpu.VMEM((DEVS, 32, VERT), BF16),
+    pltpu.SemaphoreType.DMA((2,)),
+]
+
+
+def send_kernel(req_ref, field_ref, out_ref, slab, low, high, both, sems):
+    slab[...] = field_ref[:, :MAIN, :]
+
+    def put(d, carry):
+        for k in range(CAP):
+            send_main(slab, req_ref[2 * d + k], 2 * d + k, out_ref, sems.at[0])
+        return carry
+
+    lax.fori_loop(0, DEVS, put, 0, unroll=8)
+    for b in range(BLK):
+        low[b], high[b] = ends(field_ref[b, MAIN:, :])
+    send_ends(req_ref, low, high, both, out_ref, sems)
 
 
 def pack_field(req, field):
@@ -161,12 +262,12 @@
         send_kernel,
         grid_spec=grid_spec(
             1,
-            ROWS // PACK,
+            1,
             [whole(BLK, CH, VERT)],
-            pl.BlockSpec((PACK, CHP, VERT), lambda i, *_: (i, 0, 0)),
-            [pltpu.VMEM((BLK, CHP, VERT), BF16)],
-        ),
-        out_shape=pltpu.HBM((ROWS, CHP, VERT), BF16),
+            pl.BlockSpec(memory_space=pltpu.HBM),
+            [pltpu.VMEM((BLK, MAIN, VERT), BF16), *SEND_SCRATCH],
+        ),
+        out_shape=pltpu.HBM((DEVS, WIRE, VERT), BF16),
         cost_estimate=cost(1e7),
         compiler_params=params(8),
         name="pack_field",
@@ -349,73 +450,122 @@
 
 
 def far_kernel(
-    idx_ref, got_ref, tiles_ref, near_ref, albedo_ref, area_ref, out_ref, energy_ref, rows, field, tiles, sems
+    idx_ref,
+    req_ref,
+    order_ref,
+    start_ref,
+    got_ref,
+    tiles_ref,
+    near_ref,
+    albedo_ref,
+    area_ref,
+    out_ref,
+    energy_ref,
+    *more,
+    send,
 ):
-    s = pl.program_id(0)
+    if send:
+        wire_ref, rows, field, last, tiles, sems, slab, low, high, both, out_sems = more
+    else:
+        rows, field, last, tiles, sems = more
+    ahead = 3
+    arrived = pltpu.make_async_copy(got_ref, field.at[:, pl.ds(0, WIRE)], sems.at[BLK])
+    arrived.start()
 
     def copies(at):
         return pltpu.make_async_copy(tiles_ref.at[at], tiles.at[at], sems.at[at])
 
-    @pl.when(s == 0)
-    def _():
-        whole_field = pltpu.make_async_copy(got_ref, field, sems.at[BLK])
-        whole_field.start()
-        for at in range(BLK):
-            copies(at).start()
-        whole_field.wait()
-
-    copies(s).wait()
-    for j in range(FAR):
-        rows[:, j * VERT : (j + 1) * VERT] = field[idx_ref[s * PAIRS + NEAR + j]]
-    total = near_ref[0] + product(rows[...], tiles[s])[:CH]
+    for at in range(ahead):
+        copies(at).start()
+    arrived.wait()
+    for at in range(ahead, BLK):
+        copies(at).start()
+
+    def split(d, carry):
+        both_ends = field[d, 2 * MAIN : 2 * MAIN + 32]
+        last[2 * d] = both_ends[0:16]
+        last[2 * d + 1] = both_ends[SECOND : SECOND + 16]
+        return carry
+
+    lax.fori_loop(0, DEVS, split, 0, unroll=8)
     channel = lax.broadcasted_iota(I32, (CH, VERT), 0)
-    shade = jnp.where(
-        channel < CH // COLORS,
-        albedo_ref[0, 0:1, :],
-        jnp.where(channel < 2 * (CH // COLORS), albedo_ref[0, 1:2, :], albedo_ref[0, 2:3, :]),
-    )
-    bounce = total * shade
-    out_ref[0] = bounce.astype(BF16)
-    share = jnp.sum(area_ref[0] * bounce * bounce, axis=0, keepdims=True)
-
-    @pl.when(s == 0)
-    def _():
-        energy_ref[...] = share
-
-    @pl.when(s > 0)
-    def _():
-        energy_ref[...] = energy_ref[...] + share
-
-
-def far_bounce(idx, got, tiles, near, albedo, area):
-    return pl.pallas_call(
-        far_kernel,
+
+    def gather(s, rows):
+        for j in range(FAR):
+            row = idx_ref[s * PAIRS + NEAR + j]
+            cols = slice(j * VERT, (j + 1) * VERT)
+            at = pl.multiple_of((row & 1) * MAIN, MAIN)
+            rows[0:MAIN, cols] = field[row >> 1, pl.ds(at, MAIN)]
+            rows[MAIN : MAIN + 16, cols] = last[row]
+
+    def finish(s, got):
+        total = near_ref[s] + got[:CH]
+        shade = jnp.where(
+            channel < CH // COLORS,
+            albedo_ref[s, 0:1, :],
+            jnp.where(channel < 2 * (CH // COLORS), albedo_ref[s, 1:2, :], albedo_ref[s, 2:3, :]),
+        )
+        bounce = total * shade
+        rounded = bounce.astype(BF16)
+        out_ref[s] = rounded
+        if send:
+            slab[s] = rounded[:MAIN]
+            low[s], high[s] = ends(rounded[MAIN:])
+        return jnp.sum(area_ref[s] * bounce * bounce, axis=0, keepdims=True)
+
+    def group(h, energy):
+        these = [h * GROUP + i for i in range(GROUP)]
+        for s in these:
+            copies(s).wait()
+        for i, s in enumerate(these):
+            gather(s, rows.at[i])
+        results = [product(rows[i], tiles[s]) for i, s in enumerate(these)]
+        for s, got in zip(these, results):
+            energy = energy + finish(s, got)
+        if send:
+
+            def push(i, carry):
+                send_main(slab, req_ref[order_ref[i]], order_ref[i], wire_ref, out_sems.at[0])
+                return carry
+
+            lax.fori_loop(start_ref[h * GROUP], start_ref[(h + 1) * GROUP], push, 0)
+        return energy
+
+    energy_ref[...] = lax.fori_loop(0, BLK // GROUP, group, jnp.zeros((1, VERT), F32))
+    if send:
+        send_ends(req_ref, low, high, both, wire_ref, out_sems)
+
+
+GROUP = 2
+
+
+def far_bounce(idx, req, order, start, got, tiles, near, albedo, area, send):
+    hbm = pl.BlockSpec(memory_space=pltpu.HBM)
+    return pl.pallas_call(
+        functools.partial(far_kernel, send=send),
         grid_spec=grid_spec(
+            4,
             1,
-            BLK,
+            [hbm, hbm, whole(BLK, CH, VERT), whole(BLK, COLORS, VERT), whole(BLK, 1, VERT)],
+            [whole(BLK, CH, VERT), whole(1, VERT)] + [hbm] * send,
             [
-                pl.BlockSpec(memory_space=pltpu.HBM),
-                pl.BlockSpec(memory_space=pltpu.HBM),
-                slot(CH, VERT),
-                slot(COLORS, VERT),
-                slot(1, VERT),
-            ],
-            [slot(CH, VERT), whole(1, VERT)],
-            [
-                pltpu.VMEM((CHP, FAR * VERT), BF16),
-                pltpu.VMEM((ROWS, CHP, VERT), BF16),
+                pltpu.VMEM((GROUP, MAIN + 16, FAR * VERT), BF16),
+                pltpu.VMEM((DEVS, WIRE + 8, VERT), BF16),
+                pltpu.VMEM((ROWS, 16, VERT), BF16),
                 pltpu.VMEM((BLK, FAR * VERT, VERT), BF16),
                 pltpu.SemaphoreType.DMA((BLK + 1,)),
-            ],
-        ),
-        out_shape=(
+            ]
+            + [pltpu.VMEM((BLK, MAIN, VERT), BF16), *SEND_SCRATCH] * send,
+        ),
+        out_shape=[
             jax.ShapeDtypeStruct((BLK, CH, VERT), BF16),
             jax.ShapeDtypeStruct((1, VERT), F32),
-        ),
+        ]
+        + [pltpu.HBM((DEVS, WIRE, VERT), BF16)] * send,
         cost_estimate=cost(5e8),
         compiler_params=params(),
-        name="far_bounce",
-    )(idx, got, in_hbm(tiles), near, albedo, area)
+        name="far_bounce_one" if send else "far_bounce_two",
+    )(idx, req, order, start, in_hbm(got), in_hbm(tiles), near, albedo, area)
 
 
 def swap(value):
@@ -426,15 +576,21 @@
     area_row = area.reshape(BLK, 1, VERT)
     idx, need = find_indices(pairs, home)
     idx = idx.reshape(-1)
+    sources = source_table(positions, normals, area_row)
     asked = swap(need).reshape(-1)
+    geometry = swap(pack_geometry(asked, sources))
+    got_one = swap(pack_field(asked, transfer))
     near_tiles, near_one = near_first(idx, transfer, positions, normals, area_row)
-    geometry = swap(pack_geometry(asked, positions, normals, area_row))
-    got_one = swap(pack_field(asked, transfer))
     tiles = far_tiles(idx, geometry, positions, normals)
-    bounce_one, share_one = far_bounce(idx, got_one, tiles, near_one, albedo, area_row)
-    got_two = swap(pack_field(asked, bounce_one))
+    lists = invert(asked)
+    bounce_one, share_one, wire = far_bounce(
+        idx, asked, *lists, got_one, tiles, near_one, albedo, area_row, True
+    )
+    got_two = swap(wire)
     near_two = near_again(idx, bounce_one, near_tiles)
-    bounce_two, share_two = far_bounce(idx, got_two, tiles, near_two, albedo, area_row)
+    bounce_two, share_two = far_bounce(
+        idx, asked, *lists, got_two, tiles, near_two, albedo, area_row, False
+    )
     shares = jnp.concatenate([share_one, share_two], axis=0)
     shares = swap(jnp.broadcast_to(shares[None], (DEVS, 2, VERT)))
     energies = jnp.sum(shares, axis=(0, 2)) * (1.0 / (DEVS * BLK * VERT * CH))

time: 225 us -> 214 us (0.951)
  waiting for transfers between devices: 106 us -> 94.2 us
  Pallas kernels: 75.8 us -> 78.6 us
    all_to_all x5, waiting for transfers between devices: 106 us -> 94.2 us  [swap(): return lax.all_to_all(value, AXES, split_axis=0, concat_axis=0, tiled=True)]
    pallas_call x5 -> x6, Pallas kernels: 30.3 us -> 32.3 us  [the longest x2 20.6 us: far_bounce(): pl.pallas_call(functools.partial(far_kernel, send=send), grid_spec=grid_s...]
    unnamed x16 -> x12, local copies, waits for them, and re-layouts: 6.26 us -> 4.87 us
  transfers between devices with their start and end apart: 5 -> 5, of which waited for: 5 -> 5; matrix products, arithmetic and copies ran while one was open for 2% -> 2% of each run, Pallas kernels for 22% -> 25%
where the time goes in v2:
time: 214 us
  waiting for transfers between devices  94.2 us (44%)
  Pallas kernels  78.6 us (37%)
  starting transfers between devices  32 us (15%)
  local copies, waits for them, and re-layouts  6.29 us (3%)
    all_to_all x5, waiting for transfers between devices, swap(): return lax.all_to_all(value, AXES, split_axis=0, concat_axis=0, tiled=True)  94.2 us
    all_to_all x5, starting transfers between devices, swap(): return lax.all_to_all(value, AXES, split_axis=0, concat_axis=0, tiled=True)  32 us
    pallas_call x1, Pallas kernels, far_tiles(): pl.pallas_call(far_tiles_kernel, grid_spec=grid_spec(1, BLK, [whole(ROWS,...  22.8 us
    pallas_call x2, Pallas kernels, far_bounce(): pl.pallas_call(functools.partial(far_kernel, send=send), grid_spec=grid_s...  20.6 us
    pallas_call x1, Pallas kernels, near_first(): pl.pallas_call(near_kernel, grid_spec=grid_spec(1, BLK, [whole(BLK, CH, V...  15 us
    pallas_call x1, Pallas kernels, invert(): pl.pallas_call(invert_kernel, grid_spec=grid_spec(1, 1, [], [smem, smem],...  6.76 us
    pallas_call x1, Pallas kernels, near_again(): pl.pallas_call(near_again_kernel, grid_spec=grid_spec(1, BLK, [whole(BLK,...  6.45 us
    unnamed x12, local copies, waits for them, and re-layouts  4.87 us
  transfers between devices with their start and end apart: 5, of which 5 were waited for; matrix products, arithmetic and copies ran while one was open for 2% of the time, Pallas kernels for 25%

profile of v2, /device:TPU:1, one launch (start us, length us, event | category | flops | bytes accessed | tf_op | source)
XLA Modules:
  0.0 213.5 jit_solution(3723382972089545437)
XLA Ops:
  0.6 2.0 indices.1
  2.7 11.5 %all-to-all-start = ((s32[128,1,2]{2,1,0:T(1,128)}), s32[128,1,2]{2,1,0:T(1,128)S(1)}, u32[]{:S(2)}, u32[]{:S(2)}) async-start(s32[128,1,2]{2,1,0:T(1,128)} %bitcast.2), calls=%async_computation | async-start | bytes 131072 | tf_op jit(solution)/shard_map/all_to_all | solution.py:572
  14.2 0.8 copy.62.pos_ref
  14.9 0.8 copy.63.nrm_ref
  15.7 0.7 copy-done
  16.4 7.5 %all-to-all-done = s32[128,1,2]{2,1,0:T(1,128)S(1)} async-done(((s32[128,1,2]{2,1,0:T(1,128)}), s32[128,1,2]{2,1,0:T(1,128)S(1)}, u32[]{:S(2)}, u32[]{:S(2)}) %all-to-all-start) | async-done | bytes 1056 | tf_op jit(solution)/shard_map/all_to_all | solution.py:572
  23.9 0.5 broadcast.9
  24.4 0.8 reduce.3
  25.2 0.1 reshape.24.req_ref
  25.4 1.8 pack_geometry.1
  27.2 4.3 %all-to-all-start.2 = ((bf16[256,8,128]{2,1,0:T(8,128)(2,1)}), bf16[256,8,128]{2,1,0:T(8,128)(2,1)S(1)}, u32[]{:S(2)}, u32[]{:S(2)}) async-start(bf16[256,8,128]{2,1,0:T(8,128)(2,1)} %pack_geometry.1), calls=%async_computation.2 | async-start | bytes 1048576 | tf_op jit(solution)/shard_map/all_to_all | solution.py:572
  31.5 1.1 copy.61.field_ref
  32.5 3.1 %pack_field.1 = bf16[128,152,128]{2,1,0:T(8,128)(2,1)} custom-call(s32[256]{0:T(256)S(1)} %reshape.24.req_ref, bf16[16,75,128]{2,1,0:T(8,128)(2,1)S(1)} %copy.61.field_ref), custom_call_target="tpu_custom_call" | custom-call | flops 10000000 | tf_op jit(solution)/shard_map/pack_field/pallas_call | solution.py:261
  35.7 9.9 %all-to-all-done.2.got_ref = bf16[256,8,128]{2,1,0:T(8,128)(2,1)S(1)} async-done(((bf16[256,8,128]{2,1,0:T(8,128)(2,1)}), bf16[256,8,128]{2,1,0:T(8,128)(2,1)S(1)}, u32[]{:S(2)}, u32[]{:S(2)}) %all-to-all-start.2) | async-done | bytes 524320 | tf_op jit(solution)/shard_map/all_to_all | solution.py:572
  45.6 5.1 %all-to-all-start.1 = ((bf16[128,152,128]{2,1,0:T(8,128)(2,1)}), bf16[128,152,128]{2,1,0:T(8,128)(2,1)}, u32[]{:S(2)}, u32[]{:S(2)}) async-start(bf16[128,152,128]{2,1,0:T(8,128)(2,1)} %pack_field.1), calls=%async_computation.1 | async-start | bytes 9961472 | tf_op jit(solution)/shard_map/all_to_all | solution.py:572
  50.7 0.1 reshape.23.idx_ref
  50.8 15.0 %near_first.1 = (bf16[16,2048,128]{2,1,0:T(8,128)(2,1)}, f32[16,75,128]{2,1,0:T(8,128)S(1)}) custom-call(s32[640]{0:T(1024)S(1)} %reshape.23.idx_ref, bf16[16,75,128]{2,1,0:T(8,128)(2,1)S(1)} %copy.61.field_ref, f32[16,3,128]{2,1,0:T(4,128)S(1)} %copy.62.pos_ref, f32[16,3,128]{2,1,0:T(4,128)S(1)} %copy.63.nrm_ref, f32[16,1,128]{2,1,0:T(1,128)S(1)} %bitcast.6), custom_call_target="tpu_custom_call" | custom-call | flops 600000000 | tf_op jit(solution)/shard_map/near_first/pallas_call | solution.py:359
  65.8 6.8 %invert.1 = (s32[256]{0:T(256)S(1)}, s32[17]{0:T(128)S(1)}) custom-call(s32[256]{0:T(256)S(1)} %reshape.24.req_ref), custom_call_target="tpu_custom_call" | custom-call | flops 10000000 | tf_op jit(solution)/shard_map/invert/pallas_call | solution.py:195
  72.6 22.8 %far_tiles.1.tiles_ref = bf16[16,3072,128]{2,1,0:T(8,128)(2,1)} custom-call(s32[640]{0:T(1024)S(1)} %reshape.23.idx_ref, bf16[256,8,128]{2,1,0:T(8,128)(2,1)S(1)} %all-to-all-done.2.got_ref, f32[16,3,128]{2,1,0:T(4,128)S(1)} %copy.62.pos_ref, f32[16,3,128]{2,1,0:T(4,128)S(1)} %copy.63.nrm_ref), custom_call_target="tpu_custom_call" | custom-call | flops 600000000 | tf_op jit(solution)/shard_map/far_tiles/pallas_call | solution.py:436
  95.4 15.1 %all-to-all-done.1.got_ref = bf16[128,152,128]{2,1,0:T(8,128)(2,1)} async-done(((bf16[128,152,128]{2,1,0:T(8,128)(2,1)}), bf16[128,152,128]{2,1,0:T(8,128)(2,1)}, u32[]{:S(2)}, u32[]{:S(2)}) %all-to-all-start.1) | async-done | bytes 4980768 | tf_op jit(solution)/shard_map/all_to_all | solution.py:572
  110.4 12.1 %far_bounce_one.1 = (bf16[16,75,128]{2,1,0:T(8,128)(2,1)S(1)}, f32[1,128]{1,0:T(1,128)S(1)}, bf16[128,152,128]{2,1,0:T(8,128)(2,1)}) custom-call(s32[640]{0:T(1024)S(1)} %reshape.23.idx_ref, s32[256]{0:T(256)S(1)} %reshape.24.req_ref, s32[256]{0:T(256)S(1)} %get-tuple-element.16.order_ref, s32[17]{0:T(128)S(1)} %get-tuple-element.17.start_ref, ...), custom_call_target="tpu_custom_call" | custom-call | flops 500000000 | tf_op jit(solution)/shard_map/far_bounce_one/pallas_call | solution.py:544
  122.6 5.8 %all-to-all-start.3 = ((bf16[128,152,128]{2,1,0:T(8,128)(2,1)}), bf16[128,152,128]{2,1,0:T(8,128)(2,1)}, u32[]{:S(2)}, u32[]{:S(2)}) async-start(bf16[128,152,128]{2,1,0:T(8,128)(2,1)} %get-tuple-element.20), calls=%async_computation.3 | async-start | bytes 9961472 | tf_op jit(solution)/shard_map/all_to_all | solution.py:572
  128.4 6.4 %near_again.1.near_ref = f32[16,75,128]{2,1,0:T(8,128)S(1)} custom-call(s32[640]{0:T(1024)S(1)} %reshape.23.idx_ref, bf16[16,75,128]{2,1,0:T(8,128)(2,1)S(1)} %get-tuple-element.37.field_ref, bf16[16,2048,128]{2,1,0:T(8,128)(2,1)} %get-tuple-element.21.tiles_ref), custom_call_target="tpu_custom_call" | custom-call | flops 300000000 | tf_op jit(solution)/shard_map/near_again/pallas_call | solution.py:400
  134.8 53.2 %all-to-all-done.3.got_ref = bf16[128,152,128]{2,1,0:T(8,128)(2,1)} async-done(((bf16[128,152,128]{2,1,0:T(8,128)(2,1)}), bf16[128,152,128]{2,1,0:T(8,128)(2,1)}, u32[]{:S(2)}, u32[]{:S(2)}) %all-to-all-start.3) | async-done | bytes 4980768 | tf_op jit(solution)/shard_map/all_to_all | solution.py:572
  188.0 8.5 %far_bounce_two.1 = (bf16[16,75,128]{2,1,0:T(8,128)(2,1)S(1)}, f32[1,128]{1,0:T(1,128)S(1)}) custom-call(s32[640]{0:T(1024)S(1)} %reshape.23.idx_ref, s32[256]{0:T(256)S(1)} %reshape.24.req_ref, s32[256]{0:T(256)S(1)} %get-tuple-element.16.order_ref, s32[17]{0:T(128)S(1)} %get-tuple-element.17.start_ref, bf16[128,152,128]{2,1,0:T(8,128)(2,1)} %all-to-all-done.3.got_ref, ...), custom_call_target="tpu_custom_call" | custom-call | flops 500000000 | tf_op jit(solution)/shard_map/far_bounce_two/pallas_call | solution.py:544
  196.5 0.7 broadcast_in_dim.2
  197.2 5.4 %all-to-all-start.4 = ((f32[128,2,128]{2,1,0:T(2,128)}), f32[128,2,128]{2,1,0:T(2,128)S(1)}, u32[]{:S(2)}, u32[]{:S(2)}) async-start(f32[128,2,128]{2,1,0:T(2,128)} %broadcast_in_dim.2), calls=%async_computation.4 | async-start | bytes 262144 | tf_op jit(solution)/shard_map/all_to_all | solution.py:572
  202.6 0.8 copy.72
  203.4 0.8 copy.73
  204.2 8.6 %all-to-all-done.4 = f32[128,2,128]{2,1,0:T(2,128)S(1)} async-done(((f32[128,2,128]{2,1,0:T(2,128)}), f32[128,2,128]{2,1,0:T(2,128)S(1)}, u32[]{:S(2)}, u32[]{:S(2)}) %all-to-all-start.4) | async-done | bytes 131104 | tf_op jit(solution)/shard_map/all_to_all | solution.py:572
  212.8 0.3 reduce_sum.9
  213.0 0.5 broadcast_multiply_fusion
  (8 shorter events, 0.1 us)
Async XLA Ops:
  2.7 21.2 %all-to-all-start = ((s32[128,1,2]{2,1,0:T(1,128)}), s32[128,1,2]{2,1,0:T(1,128)S(1)}, u32[]{:S(2)}, u32[]{:S(2)}) async-start(s32[128,1,2]{2,1,0:T(1,128)} %bitcast.2), calls=%async_computation | async-start | bytes 131072 | tf_op jit(solution)/shard_map/all_to_all | solution.py:572
  15.7 0.7 copy-start
  27.2 18.4 %all-to-all-start.2 = ((bf16[256,8,128]{2,1,0:T(8,128)(2,1)}), bf16[256,8,128]{2,1,0:T(8,128)(2,1)S(1)}, u32[]{:S(2)}, u32[]{:S(2)}) async-start(bf16[256,8,128]{2,1,0:T(8,128)(2,1)} %pack_geometry.1), calls=%async_computation.2 | async-start | bytes 1048576 | tf_op jit(solution)/shard_map/all_to_all | solution.py:572
  35.7 15.0 %copy-start.2 = (f32[16,3,128]{2,0,1:T(8,128)S(1)}, f32[16,3,128]{2,0,1:T(8,128)}, u32[]{:S(2)}) copy-start(f32[16,3,128]{2,0,1:T(8,128)} %param.11) | copy-start | bytes 73732
  35.7 15.1 %copy-start.1 = (f32[16,128]{1,0:T(8,128)S(1)}, f32[16,128]{1,0:T(8,128)}, u32[]{:S(2)}) copy-start(f32[16,128]{1,0:T(8,128)} %param.10) | copy-start | bytes 24580
  45.6 64.8 %all-to-all-start.1 = ((bf16[128,152,128]{2,1,0:T(8,128)(2,1)}), bf16[128,152,128]{2,1,0:T(8,128)(2,1)}, u32[]{:S(2)}, u32[]{:S(2)}) async-start(bf16[128,152,128]{2,1,0:T(8,128)(2,1)} %pack_field.1), calls=%async_computation.1 | async-start | bytes 9961472 | tf_op jit(solution)/shard_map/all_to_all | solution.py:572
  122.6 65.4 %all-to-all-start.3 = ((bf16[128,152,128]{2,1,0:T(8,128)(2,1)}), bf16[128,152,128]{2,1,0:T(8,128)(2,1)}, u32[]{:S(2)}, u32[]{:S(2)}) async-start(bf16[128,152,128]{2,1,0:T(8,128)(2,1)} %get-tuple-element.20), calls=%async_computation.3 | async-start | bytes 9961472 | tf_op jit(solution)/shard_map/all_to_all | solution.py:572
  197.2 15.6 %all-to-all-start.4 = ((f32[128,2,128]{2,1,0:T(2,128)}), f32[128,2,128]{2,1,0:T(2,128)S(1)}, u32[]{:S(2)}, u32[]{:S(2)}) async-start(f32[128,2,128]{2,1,0:T(2,128)} %broadcast_in_dim.2), calls=%async_computation.4 | async-start | bytes 262144 | tf_op jit(solution)/shard_map/all_to_all | solution.py:572

commit v3 on v2

--- a/solution.py
+++ b/solution.py
@@ -125,15 +125,16 @@
 
 
 def table_kernel(pos_ref, nrm_ref, area_ref, out_ref):
-    out_ref[:, 0:3, :] = pos_ref[...]
-    out_ref[:, 3:6, :] = nrm_ref[...] * (area_ref[...] * (-1.0 / math.pi))
-    out_ref[:, 6:8, :] = jnp.ones((BLK, 2, VERT), F32)
+    scaled = nrm_ref[...] * (area_ref[...] * (-1.0 / math.pi))
+    for i in range(3):
+        both = jnp.concatenate([pos_ref[:, i : i + 1, :], scaled[:, i : i + 1, :]], axis=1)
+        out_ref[:, i] = both.astype(BF16)
 
 
 def source_table(pos, nrm, area):
     return pl.pallas_call(
         table_kernel,
-        out_shape=jax.ShapeDtypeStruct((BLK, 8, VERT), F32),
+        out_shape=jax.ShapeDtypeStruct((BLK, 3, 2, VERT), BF16),
         cost_estimate=cost(1e6),
         compiler_params=pltpu.CompilerParams(vmem_limit_bytes=8 * 1024 * 1024),
         name="source_table",
@@ -141,68 +142,23 @@
 
 
 def geometry_kernel(req_ref, table, out_ref):
-    def put(i, carry):
-        out_ref[i] = table[req_ref[i]].astype(BF16)
+    def put(d, carry):
+        for k in range(CAP):
+            out_ref[d, :, 2 * k : 2 * k + 2, :] = table[req_ref[d, 0, k]]
         return carry
 
-    lax.fori_loop(0, ROWS, put, 0, unroll=8)
+    lax.fori_loop(0, DEVS, put, 0, unroll=8)
 
 
 def pack_geometry(req, table):
     return pl.pallas_call(
         geometry_kernel,
-        grid_spec=grid_spec(1, 1, [whole(BLK, 8, VERT)], whole(ROWS, 8, VERT), []),
-        out_shape=jax.ShapeDtypeStruct((ROWS, 8, VERT), BF16),
+        grid_spec=grid_spec(1, 1, [whole(BLK, 3, 2, VERT)], whole(DEVS, 3, 4, VERT), []),
+        out_shape=jax.ShapeDtypeStruct((DEVS, 3, 4, VERT), BF16),
         cost_estimate=cost(2e6),
         compiler_params=params(8),
         name="pack_geometry",
     )(req, table)
-
-
-def invert_kernel(req_ref, order_ref, start_ref, at):
-    def clear(b, carry):
-        start_ref[b] = 0
-        return carry
-
-    lax.fori_loop(0, BLK + 1, clear, 0)
-
-    def count(i, carry):
-        b = req_ref[i] + 1
-        start_ref[b] = start_ref[b] + 1
-        return carry
-
-    lax.fori_loop(0, ROWS, count, 0)
-
-    def add(b, total):
-        at[b] = total
-        total = total + start_ref[b + 1]
-        start_ref[b + 1] = total
-        return total
-
-    lax.fori_loop(0, BLK, add, 0)
-
-    def place(i, carry):
-        b = req_ref[i]
-        order_ref[at[b]] = i
-        at[b] = at[b] + 1
-        return carry
-
-    lax.fori_loop(0, ROWS, place, 0)
-
-
-def invert(req):
-    smem = pl.BlockSpec(memory_space=pltpu.SMEM)
-    return pl.pallas_call(
-        invert_kernel,
-        grid_spec=grid_spec(1, 1, [], [smem, smem], [pltpu.SMEM((BLK,), I32)]),
-        out_shape=(
-            jax.ShapeDtypeStruct((ROWS,), I32),
-            jax.ShapeDtypeStruct((BLK + 1,), I32),
-        ),
-        cost_estimate=cost(1e7),
-        compiler_params=params(8),
-        name="invert",
-    )(req)
 
 
 def ends(last):
@@ -213,14 +169,16 @@
     return low.astype(BF16), high.astype(BF16)
 
 
-def send_main(slab, b, i, out_ref, sem):
-    at = pl.multiple_of((i & 1) * MAIN, MAIN)
-    pltpu.make_async_copy(
-        slab.at[b, pl.ds(0, MAIN)], out_ref.at[i >> 1, pl.ds(at, MAIN)], sem
-    ).start()
-
-
-def send_ends(req_ref, low, high, both, out_ref, sems):
+def send_all(req_ref, slab, low, high, both, out_ref, sems):
+    def main_rows(d, carry):
+        for k in range(CAP):
+            pltpu.make_async_copy(
+                slab.at[req_ref[2 * d + k]], out_ref.at[d, pl.ds(k * MAIN, MAIN)], sems.at[0]
+            ).start()
+        return carry
+
+    lax.fori_loop(0, DEVS, main_rows, 0, unroll=16)
+
     def put(d, carry):
         both[d] = low[req_ref[2 * d]] + high[req_ref[2 * d + 1]]
         return carry
@@ -245,16 +203,9 @@
 
 def send_kernel(req_ref, field_ref, out_ref, slab, low, high, both, sems):
     slab[...] = field_ref[:, :MAIN, :]
-
-    def put(d, carry):
-        for k in range(CAP):
-            send_main(slab, req_ref[2 * d + k], 2 * d + k, out_ref, sems.at[0])
-        return carry
-
-    lax.fori_loop(0, DEVS, put, 0, unroll=8)
     for b in range(BLK):
         low[b], high[b] = ends(field_ref[b, MAIN:, :])
-    send_ends(req_ref, low, high, both, out_ref, sems)
+    send_all(req_ref, slab, low, high, both, out_ref, sems)
 
 
 def pack_field(req, field):
@@ -422,11 +373,15 @@
 
     @pl.when(s == 0)
     def _():
-        def make(t, carry):
-            table[t] = source_rows(got_ref[t].astype(F32), FAR_TERMS)
+        def make(d, carry):
+            got = [got_ref[d, i].astype(F32) for i in range(3)]
+            ones = jnp.ones((2, VERT), F32)
+            for k in range(CAP):
+                parts = [g[2 * k : 2 * k + 1] for g in got] + [g[2 * k + 1 : 2 * k + 2] for g in got]
+                table[CAP * d + k] = source_rows(stack_rows([*parts, ones]), FAR_TERMS)
             return carry
 
-        lax.fori_loop(0, ROWS, make, 0, unroll=4)
+        lax.fori_loop(0, DEVS, make, 0, unroll=2)
 
     recv[...] = receiver_rows(pos_ref[s], nrm_ref[s], FAR_TERMS)
     fill_tiles(lambda j: idx_ref[s * PAIRS + NEAR + j], FAR, recv, table, tiles_ref)
@@ -438,7 +393,7 @@
         grid_spec=grid_spec(
             1,
             BLK,
-            [whole(ROWS, 8, VERT), whole(BLK, 3, VERT), whole(BLK, 3, VERT)],
+            [whole(DEVS, 3, 4, VERT), whole(BLK, 3, VERT), whole(BLK, 3, VERT)],
             slot(FAR * VERT, VERT),
             [pltpu.VMEM((ROWS, VERT, FAR_K), BF16), pltpu.VMEM((FAR_K, 3 * VERT), BF16)],
         ),
@@ -450,24 +405,23 @@
 
 
 def far_kernel(
-    idx_ref,
-    req_ref,
-    order_ref,
-    start_ref,
+    idx_any,
+    req_any,
     got_ref,
     tiles_ref,
     near_ref,
     albedo_ref,
     area_ref,
+    share_ref,
     out_ref,
     energy_ref,
     *more,
     send,
 ):
     if send:
-        wire_ref, rows, field, last, tiles, sems, slab, low, high, both, out_sems = more
+        wire_ref, idx_ref, req_ref, rows, field, last, tiles, sems, slab, low, high, both, out_sems = more
     else:
-        rows, field, last, tiles, sems = more
+        idx_ref, req_ref, rows, field, last, tiles, sems = more
     ahead = 3
     arrived = pltpu.make_async_copy(got_ref, field.at[:, pl.ds(0, WIRE)], sems.at[BLK])
     arrived.start()
@@ -475,8 +429,15 @@
     def copies(at):
         return pltpu.make_async_copy(tiles_ref.at[at], tiles.at[at], sems.at[at])
 
+    small = [pltpu.make_async_copy(idx_any, idx_ref, sems.at[BLK + 1])]
+    if send:
+        small.append(pltpu.make_async_copy(req_any, req_ref, sems.at[BLK + 2]))
+    for one in small:
+        one.start()
     for at in range(ahead):
         copies(at).start()
+    for one in small:
+        one.wait()
     arrived.wait()
     for at in range(ahead, BLK):
         copies(at).start()
@@ -522,50 +483,52 @@
         results = [product(rows[i], tiles[s]) for i, s in enumerate(these)]
         for s, got in zip(these, results):
             energy = energy + finish(s, got)
-        if send:
-
-            def push(i, carry):
-                send_main(slab, req_ref[order_ref[i]], order_ref[i], wire_ref, out_sems.at[0])
-                return carry
-
-            lax.fori_loop(start_ref[h * GROUP], start_ref[(h + 1) * GROUP], push, 0)
         return energy
 
-    energy_ref[...] = lax.fori_loop(0, BLK // GROUP, group, jnp.zeros((1, VERT), F32))
+    energy = lax.fori_loop(0, BLK // GROUP, group, jnp.zeros((1, VERT), F32)) * INV_COUNT
     if send:
-        send_ends(req_ref, low, high, both, wire_ref, out_sems)
+        energy_ref[...] = energy
+        send_all(req_ref, slab, low, high, both, wire_ref, out_sems)
+    else:
+        shares = jnp.concatenate([share_ref[...], energy], axis=0)
+        energy_ref[...] = jnp.broadcast_to(shares[None], (DEVS, 2, VERT))
 
 
 GROUP = 2
-
-
-def far_bounce(idx, req, order, start, got, tiles, near, albedo, area, send):
+INV_COUNT = 1.0 / (DEVS * BLK * VERT * CH)
+
+
+def far_bounce(idx, req, got, tiles, near, albedo, area, share, send):
     hbm = pl.BlockSpec(memory_space=pltpu.HBM)
+    vmem = pl.BlockSpec(memory_space=pltpu.VMEM)
+    any_space = pl.BlockSpec(memory_space=pl.ANY)
     return pl.pallas_call(
         functools.partial(far_kernel, send=send),
         grid_spec=grid_spec(
-            4,
+            0,
             1,
-            [hbm, hbm, whole(BLK, CH, VERT), whole(BLK, COLORS, VERT), whole(BLK, 1, VERT)],
-            [whole(BLK, CH, VERT), whole(1, VERT)] + [hbm] * send,
+            [any_space, any_space, hbm, hbm, vmem, vmem, vmem, vmem],
+            [vmem, vmem] + [hbm] * send,
             [
+                pltpu.SMEM((BLK * PAIRS,), I32),
+                pltpu.SMEM((ROWS,), I32),
                 pltpu.VMEM((GROUP, MAIN + 16, FAR * VERT), BF16),
                 pltpu.VMEM((DEVS, WIRE + 8, VERT), BF16),
                 pltpu.VMEM((ROWS, 16, VERT), BF16),
                 pltpu.VMEM((BLK, FAR * VERT, VERT), BF16),
-                pltpu.SemaphoreType.DMA((BLK + 1,)),
+                pltpu.SemaphoreType.DMA((BLK + 3,)),
             ]
             + [pltpu.VMEM((BLK, MAIN, VERT), BF16), *SEND_SCRATCH] * send,
         ),
         out_shape=[
             jax.ShapeDtypeStruct((BLK, CH, VERT), BF16),
-            jax.ShapeDtypeStruct((1, VERT), F32),
+            jax.ShapeDtypeStruct((1, VERT) if send else (DEVS, 2, VERT), F32),
         ]
         + [pltpu.HBM((DEVS, WIRE, VERT), BF16)] * send,
         cost_estimate=cost(5e8),
         compiler_params=params(),
         name="far_bounce_one" if send else "far_bounce_two",
-    )(idx, req, order, start, in_hbm(got), in_hbm(tiles), near, albedo, area)
+    )(idx, req, in_hbm(got), in_hbm(tiles), near, albedo, area, share)
 
 
 def swap(value):
@@ -577,23 +540,22 @@
     idx, need = find_indices(pairs, home)
     idx = idx.reshape(-1)
     sources = source_table(positions, normals, area_row)
-    asked = swap(need).reshape(-1)
+    asked = swap(need.reshape(DEVS, 1, CAP))
     geometry = swap(pack_geometry(asked, sources))
+    asked = asked.reshape(-1)
     got_one = swap(pack_field(asked, transfer))
     near_tiles, near_one = near_first(idx, transfer, positions, normals, area_row)
     tiles = far_tiles(idx, geometry, positions, normals)
-    lists = invert(asked)
+    none = jnp.zeros((1, VERT), F32)
     bounce_one, share_one, wire = far_bounce(
-        idx, asked, *lists, got_one, tiles, near_one, albedo, area_row, True
+        idx, asked, got_one, tiles, near_one, albedo, area_row, none, True
     )
     got_two = swap(wire)
     near_two = near_again(idx, bounce_one, near_tiles)
-    bounce_two, share_two = far_bounce(
-        idx, asked, *lists, got_two, tiles, near_two, albedo, area_row, False
-    )
-    shares = jnp.concatenate([share_one, share_two], axis=0)
-    shares = swap(jnp.broadcast_to(shares[None], (DEVS, 2, VERT)))
-    energies = jnp.sum(shares, axis=(0, 2)) * (1.0 / (DEVS * BLK * VERT * CH))
+    bounce_two, shares = far_bounce(
+        idx, asked, got_two, tiles, near_two, albedo, area_row, share_one, False
+    )
+    energies = jnp.sum(swap(shares), axis=(0, 2))
     return bounce_one, bounce_two, energies
 
 

time: 214 us -> 210 us (0.981)
  Pallas kernels: 78.6 us -> 71.3 us
  waiting for transfers between devices: 94.2 us -> 98 us
    pallas_call x4 -> x3, Pallas kernels: 31.4 us -> 26.1 us  [the longest x1 23.2 us: far_tiles(): pl.pallas_call(far_tiles_kernel, grid_spec=grid_spec(1, BLK, [whole(DEVS,...]
    all_to_all x5, waiting for transfers between devices: 94.2 us -> 98 us  [swap(): return lax.all_to_all(value, AXES, split_axis=0, concat_axis=0, tiled=True)]
  transfers between devices with their start and end apart: 5 -> 5, of which waited for: 5 -> 5; matrix products, arithmetic and copies ran while one was open for 2% -> 3% of each run, Pallas kernels for 25% -> 23%
where the time goes in v3:
time: 210 us; the launch traced here: 209 us
  waiting for transfers between devices  98 us (47%)
  Pallas kernels  71.3 us (34%)
  starting transfers between devices  32 us (15%)
  local copies, waits for them, and re-layouts  5.6 us (3%)
    all_to_all x5, waiting for transfers between devices, swap(): return lax.all_to_all(value, AXES, split_axis=0, concat_axis=0, tiled=True)  98 us
    all_to_all x5, starting transfers between devices, swap(): return lax.all_to_all(value, AXES, split_axis=0, concat_axis=0, tiled=True)  32 us
    pallas_call x1, Pallas kernels, far_tiles(): pl.pallas_call(far_tiles_kernel, grid_spec=grid_spec(1, BLK, [whole(DEVS,...  23.2 us
    pallas_call x2, Pallas kernels, far_bounce(): pl.pallas_call(functools.partial(far_kernel, send=send), grid_spec=grid_s...  18.8 us
    pallas_call x1, Pallas kernels, near_first(): pl.pallas_call(near_kernel, grid_spec=grid_spec(1, BLK, [whole(BLK, CH, V...  15 us
    pallas_call x1, Pallas kernels, near_again(): pl.pallas_call(near_again_kernel, grid_spec=grid_spec(1, BLK, [whole(BLK,...  6.44 us
    unnamed x12, local copies, waits for them, and re-layouts  4.87 us
  transfers between devices with their start and end apart: 5, of which 5 were waited for; matrix products, arithmetic and copies ran while one was open for 3% of the time, Pallas kernels for 23%

profile of v3, /device:TPU:1, one launch (start us, length us, event | category | flops | bytes accessed | tf_op | source)
XLA Modules:
  0.0 209.3 jit_solution(6638525097878125947)
XLA Ops:
  0.6 2.0 indices.1
  2.7 11.5 %all-to-all-start = ((s32[128,1,2]{2,1,0:T(1,128)}), s32[128,1,2]{2,1,0:T(1,128)S(1)}, u32[]{:S(2)}, u32[]{:S(2)}) async-start(s32[128,1,2]{2,1,0:T(1,128)} %bitcast.1), calls=%async_computation | async-start | bytes 131072 | tf_op jit(solution)/shard_map/all_to_all | solution.py:535
  14.2 0.8 copy.23.pos_ref
  14.9 0.8 copy.24.nrm_ref
  15.7 0.0 copy-start
  15.7 0.7 copy-done
  16.4 7.5 %all-to-all-done.req_ref = s32[128,1,2]{2,1,0:T(1,128)S(1)} async-done(((s32[128,1,2]{2,1,0:T(1,128)}), s32[128,1,2]{2,1,0:T(1,128)S(1)}, u32[]{:S(2)}, u32[]{:S(2)}) %all-to-all-start) | async-done | bytes 1056 | tf_op jit(solution)/shard_map/all_to_all | solution.py:535
  23.9 2.9 %pack_geometry.1 = bf16[128,3,4,128]{3,2,1,0:T(4,128)(2,1)} custom-call(s32[128,1,2]{2,1,0:T(1,128)S(1)} %all-to-all-done.req_ref, bf16[16,3,2,128]{3,2,1,0:T(2,128)(2,1)S(1)} %source_table.1.table), custom_call_target="tpu_custom_call" | custom-call | flops 2000000 | tf_op jit(solution)/shard_map/pack_geometry/pallas_call | solution.py:154
  26.8 4.3 %all-to-all-start.2 = ((bf16[128,3,4,128]{3,2,1,0:T(4,128)(2,1)}), bf16[128,3,4,128]{3,2,1,0:T(4,128)(2,1)S(1)}, u32[]{:S(2)}, u32[]{:S(2)}) async-start(bf16[128,3,4,128]{3,2,1,0:T(4,128)(2,1)} %pack_geometry.1), calls=%async_computation.2 | async-start | bytes 786432 | tf_op jit(solution)/shard_map/all_to_all | solution.py:535
  31.1 1.1 copy.22.field_ref
  32.2 0.5 broadcast.3
  32.7 0.8 reduce.3
  33.5 0.1 reshape.24.req_ref.req_any
  33.6 2.9 %pack_field.1 = bf16[128,152,128]{2,1,0:T(8,128)(2,1)} custom-call(s32[256]{0:T(256)S(1)} %reshape.24.req_ref.req_any, bf16[16,75,128]{2,1,0:T(8,128)(2,1)S(1)} %copy.22.field_ref), custom_call_target="tpu_custom_call" | custom-call | flops 10000000 | tf_op jit(solution)/shard_map/pack_field/pallas_call | solution.py:212
  36.5 0.0 copy-start.2
  36.5 0.0 copy-start.1
  36.5 7.4 %all-to-all-done.2.got_ref = bf16[128,3,4,128]{3,2,1,0:T(4,128)(2,1)S(1)} async-done(((bf16[128,3,4,128]{3,2,1,0:T(4,128)(2,1)}), bf16[128,3,4,128]{3,2,1,0:T(4,128)(2,1)S(1)}, u32[]{:S(2)}, u32[]{:S(2)}) %all-to-all-start.2) | async-done | bytes 393248 | tf_op jit(solution)/shard_map/all_to_all | solution.py:535
  43.9 5.0 %all-to-all-start.1 = ((bf16[128,152,128]{2,1,0:T(8,128)(2,1)}), bf16[128,152,128]{2,1,0:T(8,128)(2,1)}, u32[]{:S(2)}, u32[]{:S(2)}) async-start(bf16[128,152,128]{2,1,0:T(8,128)(2,1)} %pack_field.1), calls=%async_computation.1 | async-start | bytes 9961472 | tf_op jit(solution)/shard_map/all_to_all | solution.py:535
  49.0 0.1 reshape.22.idx_ref.idx_any
  49.1 15.0 %near_first.1 = (bf16[16,2048,128]{2,1,0:T(8,128)(2,1)}, f32[16,75,128]{2,1,0:T(8,128)S(1)}) custom-call(s32[640]{0:T(1024)S(1)} %reshape.22.idx_ref.idx_any, bf16[16,75,128]{2,1,0:T(8,128)(2,1)S(1)} %copy.22.field_ref, f32[16,3,128]{2,1,0:T(4,128)S(1)} %copy.23.pos_ref, f32[16,3,128]{2,1,0:T(4,128)S(1)} %copy.24.nrm_ref, f32[16,1,128]{2,1,0:T(1,128)S(1)} %bitcast.4), custom_call_target="tpu_custom_call" | custom-call | flops 600000000 | tf_op jit(solution)/shard_map/near_first/pallas_call | solution.py:310
  64.1 23.2 %far_tiles.1.tiles_ref = bf16[16,3072,128]{2,1,0:T(8,128)(2,1)} custom-call(s32[640]{0:T(1024)S(1)} %reshape.22.idx_ref.idx_any, bf16[128,3,4,128]{3,2,1,0:T(4,128)(2,1)S(1)} %all-to-all-done.2.got_ref, f32[16,3,128]{2,1,0:T(4,128)S(1)} %copy.23.pos_ref, f32[16,3,128]{2,1,0:T(4,128)S(1)} %copy.24.nrm_ref), custom_call_target="tpu_custom_call" | custom-call | flops 600000000 | tf_op jit(solution)/shard_map/far_tiles/pallas_call | solution.py:391
  87.3 21.4 %all-to-all-done.1.got_ref = bf16[128,152,128]{2,1,0:T(8,128)(2,1)} async-done(((bf16[128,152,128]{2,1,0:T(8,128)(2,1)}), bf16[128,152,128]{2,1,0:T(8,128)(2,1)}, u32[]{:S(2)}, u32[]{:S(2)}) %all-to-all-start.1) | async-done | bytes 4980768 | tf_op jit(solution)/shard_map/all_to_all | solution.py:535
  108.7 10.2 %far_bounce_one.1 = (bf16[16,75,128]{2,1,0:T(8,128)(2,1)S(1)}, f32[1,128]{1,0:T(1,128)S(1)}, bf16[128,152,128]{2,1,0:T(8,128)(2,1)}) custom-call(s32[640]{0:T(1024)S(1)} %reshape.22.idx_ref.idx_any, s32[256]{0:T(256)S(1)} %reshape.24.req_ref.req_any, bf16[128,152,128]{2,1,0:T(8,128)(2,1)} %all-to-all-done.1.got_ref, ...), custom_call_target="tpu_custom_call" | custom-call | flops 500000000 | tf_op jit(solution)/shard_map/far_bounce_one/pallas_call | solution.py:505
  118.9 5.8 %all-to-all-start.3 = ((bf16[128,152,128]{2,1,0:T(8,128)(2,1)}), bf16[128,152,128]{2,1,0:T(8,128)(2,1)}, u32[]{:S(2)}, u32[]{:S(2)}) async-start(bf16[128,152,128]{2,1,0:T(8,128)(2,1)} %get-tuple-element.16), calls=%async_computation.3 | async-start | bytes 9961472 | tf_op jit(solution)/shard_map/all_to_all | solution.py:535
  124.7 6.4 %near_again.1.near_ref = f32[16,75,128]{2,1,0:T(8,128)S(1)} custom-call(s32[640]{0:T(1024)S(1)} %reshape.22.idx_ref.idx_any, bf16[16,75,128]{2,1,0:T(8,128)(2,1)S(1)} %get-tuple-element.24.field_ref, bf16[16,2048,128]{2,1,0:T(8,128)(2,1)} %get-tuple-element.17.tiles_ref), custom_call_target="tpu_custom_call" | custom-call | flops 300000000 | tf_op jit(solution)/shard_map/near_again/pallas_call | solution.py:351
  131.2 53.2 %all-to-all-done.3.got_ref = bf16[128,152,128]{2,1,0:T(8,128)(2,1)} async-done(((bf16[128,152,128]{2,1,0:T(8,128)(2,1)}), bf16[128,152,128]{2,1,0:T(8,128)(2,1)}, u32[]{:S(2)}, u32[]{:S(2)}) %all-to-all-start.3) | async-done | bytes 4980768 | tf_op jit(solution)/shard_map/all_to_all | solution.py:535
  184.3 8.6 %far_bounce_two.1 = (bf16[16,75,128]{2,1,0:T(8,128)(2,1)S(1)}, f32[128,2,128]{2,1,0:T(2,128)}) custom-call(s32[640]{0:T(1024)S(1)} %reshape.22.idx_ref.idx_any, s32[256]{0:T(256)S(1)} %reshape.24.req_ref.req_any, bf16[128,152,128]{2,1,0:T(8,128)(2,1)} %all-to-all-done.3.got_ref, bf16[16,3072,128]{2,1,0:T(8,128)(2,1)} %far_tiles.1.tiles_ref, ...), custom_call_target="tpu_custom_call" | custom-call | flops 500000000 | tf_op jit(solution)/shard_map/far_bounce_two/pallas_call | solution.py:505
  192.9 5.4 %all-to-all-start.4 = ((f32[128,2,128]{2,1,0:T(2,128)}), f32[128,2,128]{2,1,0:T(2,128)S(1)}, u32[]{:S(2)}, u32[]{:S(2)}) async-start(f32[128,2,128]{2,1,0:T(2,128)} %get-tuple-element.20), calls=%async_computation.4 | async-start | bytes 262144 | tf_op jit(solution)/shard_map/all_to_all | solution.py:535
  198.3 0.8 copy.32
  199.1 0.8 copy.33
  199.9 8.6 %all-to-all-done.4 = f32[128,2,128]{2,1,0:T(2,128)S(1)} async-done(((f32[128,2,128]{2,1,0:T(2,128)}), f32[128,2,128]{2,1,0:T(2,128)S(1)}, u32[]{:S(2)}, u32[]{:S(2)}) %all-to-all-start.4) | async-done | bytes 131104 | tf_op jit(solution)/shard_map/all_to_all | solution.py:535
  208.5 0.8 reduce_sum.9
  (5 shorter events, 0.1 us)
Async XLA Ops:
  2.7 21.2 %all-to-all-start = ((s32[128,1,2]{2,1,0:T(1,128)}), s32[128,1,2]{2,1,0:T(1,128)S(1)}, u32[]{:S(2)}, u32[]{:S(2)}) async-start(s32[128,1,2]{2,1,0:T(1,128)} %bitcast.1), calls=%async_computation | async-start | bytes 131072 | tf_op jit(solution)/shard_map/all_to_all | solution.py:535
  15.7 0.7 copy-start
  26.8 17.1 %all-to-all-start.2 = ((bf16[128,3,4,128]{3,2,1,0:T(4,128)(2,1)}), bf16[128,3,4,128]{3,2,1,0:T(4,128)(2,1)S(1)}, u32[]{:S(2)}, u32[]{:S(2)}) async-start(bf16[128,3,4,128]{3,2,1,0:T(4,128)(2,1)} %pack_geometry.1), calls=%async_computation.2 | async-start | bytes 786432 | tf_op jit(solution)/shard_map/all_to_all | solution.py:535
  36.5 12.4 %copy-start.2 = (f32[16,3,128]{2,0,1:T(8,128)S(1)}, f32[16,3,128]{2,0,1:T(8,128)}, u32[]{:S(2)}) copy-start(f32[16,3,128]{2,0,1:T(8,128)} %param.11) | copy-start | bytes 73732
  36.5 12.5 %copy-start.1 = (f32[16,128]{1,0:T(8,128)S(1)}, f32[16,128]{1,0:T(8,128)}, u32[]{:S(2)}) copy-start(f32[16,128]{1,0:T(8,128)} %param.10) | copy-start | bytes 24580
  43.9 64.8 %all-to-all-start.1 = ((bf16[128,152,128]{2,1,0:T(8,128)(2,1)}), bf16[128,152,128]{2,1,0:T(8,128)(2,1)}, u32[]{:S(2)}, u32[]{:S(2)}) async-start(bf16[128,152,128]{2,1,0:T(8,128)(2,1)} %pack_field.1), calls=%async_computation.1 | async-start | bytes 9961472 | tf_op jit(solution)/shard_map/all_to_all | solution.py:535
  118.9 65.4 %all-to-all-start.3 = ((bf16[128,152,128]{2,1,0:T(8,128)(2,1)}), bf16[128,152,128]{2,1,0:T(8,128)(2,1)}, u32[]{:S(2)}, u32[]{:S(2)}) async-start(bf16[128,152,128]{2,1,0:T(8,128)(2,1)} %get-tuple-element.16), calls=%async_computation.3 | async-start | bytes 9961472 | tf_op jit(solution)/shard_map/all_to_all | solution.py:535
  192.9 15.6 %all-to-all-start.4 = ((f32[128,2,128]{2,1,0:T(2,128)}), f32[128,2,128]{2,1,0:T(2,128)S(1)}, u32[]{:S(2)}, u32[]{:S(2)}) async-start(f32[128,2,128]{2,1,0:T(2,128)} %get-tuple-element.20), calls=%async_computation.4 | async-start | bytes 262144 | tf_op jit(solution)/shard_map/all_to_all | solution.py:535

commit v4 on v3

--- a/solution.py
+++ b/solution.py
@@ -44,66 +44,87 @@
     return pl.CostEstimate(flops=int(flops), bytes_accessed=int(read), transcendentals=0)
 
 
-def index_kernel(pairs_hbm, home_hbm, idx_ref, req_ref, pairs_ref, home_ref, sems):
+TOGETHER = 4
+
+
+def home_parts(home):
+    return jnp.concatenate([home >> 4, home & 15], axis=0).astype(F32).astype(BF16)
+
+
+def look_up(both, blocks):
+    wide = blocks.shape[1]
+    sub = lax.broadcasted_iota(I32, (VERT, wide), 0)
+    hot = jnp.where(sub == (blocks & 127), 1.0, 0.0).astype(BF16)
+    got = jnp.dot(both, hot, preferred_element_type=F32)
+    here = lax.broadcasted_iota(I32, (16, wide), 0) == (blocks >> 7)
+    owner = jnp.sum(jnp.where(here, got[:16], 0.0), axis=0, keepdims=True)
+    local = jnp.sum(jnp.where(here, got[16:], 0.0), axis=0, keepdims=True)
+    return owner, local
+
+
+def request_kernel(pairs_hbm, home_hbm, req_ref, pairs_ref, home_ref, sems):
     first = pltpu.make_async_copy(pairs_hbm, pairs_ref, sems.at[0])
     second = pltpu.make_async_copy(home_hbm, home_ref, sems.at[1])
     first.start()
     second.start()
     first.wait()
     second.wait()
-    home = home_ref[...]
-    both = jnp.concatenate([home >> 4, home & 15], axis=0).astype(F32).astype(BF16)
-    pairs = pairs_ref[...]
-    low = pairs & 127
-    high = pairs >> 7
-    sub = lax.broadcasted_iota(I32, (VERT, PAIRS), 0)
-    sub_f = sub.astype(F32)
-    sub16 = lax.broadcasted_iota(I32, (16, PAIRS), 0)
-    lane = lax.broadcasted_iota(I32, (VERT, PAIRS), 1)
-    lane_row = lax.broadcasted_iota(I32, (1, PAIRS), 1)
-    is_far = lane >= NEAR
-    owners, locals_ = [], []
-    least = jnp.full((VERT, PAIRS), 99.0, F32)
-    most = jnp.full((VERT, PAIRS), -1.0, F32)
-    for s in range(BLK):
-        hot = jnp.where(sub == low[s : s + 1, :], 1.0, 0.0).astype(BF16)
-        got = jnp.dot(both, hot, preferred_element_type=F32)
-        here = sub16 == high[s : s + 1, :]
-        owner = jnp.sum(jnp.where(here, got[:16], 0.0), axis=0, keepdims=True)
-        local = jnp.sum(jnp.where(here, got[16:], 0.0), axis=0, keepdims=True)
-        owners.append(owner)
-        locals_.append(local)
-        same = (sub_f == owner) & is_far
+    both = home_parts(home_ref[...])
+    far = pairs_ref[...][:, NEAR:]
+    wide = TOGETHER * FAR
+    device = lax.broadcasted_iota(I32, (VERT, wide), 0).astype(F32)
+    least = jnp.full((VERT, wide), 99.0, F32)
+    most = jnp.full((VERT, wide), -1.0, F32)
+    for g in range(BLK // TOGETHER):
+        rows = [far[g * TOGETHER + i : g * TOGETHER + i + 1] for i in range(TOGETHER)]
+        owner, local = look_up(both, jnp.concatenate(rows, axis=1))
+        same = device == owner
         least = jnp.minimum(least, jnp.where(same, local, 99.0))
         most = jnp.maximum(most, jnp.where(same, local, -1.0))
     lo = jnp.min(least, axis=1, keepdims=True)
     hi = jnp.max(most, axis=1, keepdims=True)
-    for s in range(BLK):
-        first = jnp.sum(jnp.where(sub_f == owners[s], lo, 0.0), axis=0, keepdims=True)
-        far_row = owners[s] * 2.0 + jnp.where(locals_[s] == first, 0.0, 1.0)
-        idx_ref[s : s + 1, :] = jnp.where(lane_row < NEAR, locals_[s], far_row).astype(I32)
     used = hi >= 0.0
     req_ref[:, 0:1] = jnp.where(used, lo, 0.0).astype(I32)
     req_ref[:, 1:2] = jnp.where(used, hi, 0.0).astype(I32)
 
 
-def find_indices(pairs, home):
-    return pl.pallas_call(
-        index_kernel,
-        out_shape=(
-            jax.ShapeDtypeStruct((BLK, PAIRS), I32),
-            jax.ShapeDtypeStruct((DEVS, CAP), I32),
-        ),
+def find_requests(pairs, home):
+    return pl.pallas_call(
+        request_kernel,
+        out_shape=jax.ShapeDtypeStruct((DEVS, CAP), I32),
         in_specs=[pl.BlockSpec(memory_space=pltpu.HBM), pl.BlockSpec(memory_space=pltpu.HBM)],
         scratch_shapes=[
             pltpu.VMEM((BLK, PAIRS), I32),
             pltpu.VMEM((BLK, VERT), I32),
             pltpu.SemaphoreType.DMA((2,)),
         ],
+        cost_estimate=cost(2e6),
+        compiler_params=pltpu.CompilerParams(vmem_limit_bytes=8 * 1024 * 1024),
+        name="requests",
+    )(in_hbm(pairs), in_hbm(home))
+
+
+def index_kernel(pairs_ref, home_ref, req_ref, idx_ref):
+    both = home_parts(home_ref[...])
+    pairs = pairs_ref[...]
+    device = lax.broadcasted_iota(I32, (VERT, PAIRS), 0).astype(F32)
+    lane = lax.broadcasted_iota(I32, (1, PAIRS), 1)
+    lo = req_ref[:, 0:1].astype(F32)
+    for s in range(BLK):
+        owner, local = look_up(both, pairs[s : s + 1, :])
+        first = jnp.sum(jnp.where(device == owner, lo, 0.0), axis=0, keepdims=True)
+        far_row = owner * 2.0 + jnp.where(local == first, 0.0, 1.0)
+        idx_ref[s : s + 1, :] = jnp.where(lane < NEAR, local, far_row).astype(I32)
+
+
+def find_indices(pairs, home, need):
+    return pl.pallas_call(
+        index_kernel,
+        out_shape=jax.ShapeDtypeStruct((BLK, PAIRS), I32),
         cost_estimate=cost(4e6),
         compiler_params=pltpu.CompilerParams(vmem_limit_bytes=8 * 1024 * 1024),
         name="indices",
-    )(in_hbm(pairs), in_hbm(home.reshape(BLK, VERT)))
+    )(pairs, home, need)
 
 
 def whole(*shape):
@@ -422,7 +443,7 @@
         wire_ref, idx_ref, req_ref, rows, field, last, tiles, sems, slab, low, high, both, out_sems = more
     else:
         idx_ref, req_ref, rows, field, last, tiles, sems = more
-    ahead = 3
+    ahead = 5
     arrived = pltpu.make_async_copy(got_ref, field.at[:, pl.ds(0, WIRE)], sems.at[BLK])
     arrived.start()
 
@@ -537,8 +558,9 @@
 
 def body(transfer, positions, normals, area, albedo, pairs, home):
     area_row = area.reshape(BLK, 1, VERT)
-    idx, need = find_indices(pairs, home)
-    idx = idx.reshape(-1)
+    home = home.reshape(BLK, VERT)
+    need = find_requests(pairs, home)
+    idx = find_indices(pairs, home, need).reshape(-1)
     sources = source_table(positions, normals, area_row)
     asked = swap(need.reshape(DEVS, 1, CAP))
     geometry = swap(pack_geometry(asked, sources))

time: 210 us -> 209 us (level)
    unnamed x12 -> x16, local copies, waits for them, and re-layouts: 4.87 us -> 4.89 us
where the time goes in v4:
time: 209 us; the launch traced here: 208 us
  waiting for transfers between devices  96.8 us (46%)
  Pallas kernels  71.6 us (34%)
  starting transfers between devices  32 us (15%)
  local copies, waits for them, and re-layouts  5.62 us (3%)
    all_to_all x5, waiting for transfers between devices, swap(): return lax.all_to_all(value, AXES, split_axis=0, concat_axis=0, tiled=True)  96.8 us
    all_to_all x5, starting transfers between devices, swap(): return lax.all_to_all(value, AXES, split_axis=0, concat_axis=0, tiled=True)  32 us
    pallas_call x1, Pallas kernels, far_tiles(): pl.pallas_call(far_tiles_kernel, grid_spec=grid_spec(1, BLK, [whole(DEVS,...  23.2 us
    pallas_call x2, Pallas kernels, far_bounce(): pl.pallas_call(functools.partial(far_kernel, send=send), grid_spec=grid_s...  18.2 us
    pallas_call x1, Pallas kernels, near_first(): pl.pallas_call(near_kernel, grid_spec=grid_spec(1, BLK, [whole(BLK, CH, V...  15 us
    pallas_call x1, Pallas kernels, near_again(): pl.pallas_call(near_again_kernel, grid_spec=grid_spec(1, BLK, [whole(BLK,...  6.43 us
    unnamed x16, local copies, waits for them, and re-layouts  4.89 us
  transfers between devices with their start and end apart: 5, of which 5 were waited for; matrix products, arithmetic and copies ran while one was open for 3% of the time, Pallas kernels for 23%

profile of v4, /device:TPU:1, one launch (start us, length us, event | category | flops | bytes accessed | tf_op | source)
XLA Modules:
  0.0 208.4 jit_solution(3416122641113157634)
XLA Ops:
  0.6 1.7 requests.1.req_ref
  2.4 11.5 %all-to-all-start = ((s32[128,1,2]{2,1,0:T(1,128)}), s32[128,1,2]{2,1,0:T(1,128)S(1)}, u32[]{:S(2)}, u32[]{:S(2)}) async-start(s32[128,1,2]{2,1,0:T(1,128)} %bitcast.1), calls=%async_computation | async-start | bytes 131072 | tf_op jit(solution)/shard_map/all_to_all | solution.py:556
  13.9 0.8 copy.23.pos_ref
  14.6 0.8 copy.24.nrm_ref
  15.4 0.7 copy-done
  16.1 7.5 %all-to-all-done.req_ref = s32[128,1,2]{2,1,0:T(1,128)S(1)} async-done(((s32[128,1,2]{2,1,0:T(1,128)}), s32[128,1,2]{2,1,0:T(1,128)S(1)}, u32[]{:S(2)}, u32[]{:S(2)}) %all-to-all-start) | async-done | bytes 1056 | tf_op jit(solution)/shard_map/all_to_all | solution.py:556
  23.6 2.9 %pack_geometry.1 = bf16[128,3,4,128]{3,2,1,0:T(4,128)(2,1)} custom-call(s32[128,1,2]{2,1,0:T(1,128)S(1)} %all-to-all-done.req_ref, bf16[16,3,2,128]{3,2,1,0:T(2,128)(2,1)S(1)} %source_table.1.table), custom_call_target="tpu_custom_call" | custom-call | flops 2000000 | tf_op jit(solution)/shard_map/pack_geometry/pallas_call | solution.py:175
  26.5 4.3 %all-to-all-start.2 = ((bf16[128,3,4,128]{3,2,1,0:T(4,128)(2,1)}), bf16[128,3,4,128]{3,2,1,0:T(4,128)(2,1)S(1)}, u32[]{:S(2)}, u32[]{:S(2)}) async-start(bf16[128,3,4,128]{3,2,1,0:T(4,128)(2,1)} %pack_geometry.1), calls=%async_computation.2 | async-start | bytes 786432 | tf_op jit(solution)/shard_map/all_to_all | solution.py:556
  30.8 1.1 copy.22.field_ref
  31.8 0.5 broadcast.3
  32.3 0.8 reduce.3
  33.2 0.1 reshape.24.req_ref.req_any
  33.3 2.9 %pack_field.1 = bf16[128,152,128]{2,1,0:T(8,128)(2,1)} custom-call(s32[256]{0:T(256)S(1)} %reshape.24.req_ref.req_any, bf16[16,75,128]{2,1,0:T(8,128)(2,1)S(1)} %copy.22.field_ref), custom_call_target="tpu_custom_call" | custom-call | flops 10000000 | tf_op jit(solution)/shard_map/pack_field/pallas_call | solution.py:233
  36.2 0.0 copy-start.4
  36.2 0.0 copy-start.2
  36.2 7.3 %all-to-all-done.2.got_ref = bf16[128,3,4,128]{3,2,1,0:T(4,128)(2,1)S(1)} async-done(((bf16[128,3,4,128]{3,2,1,0:T(4,128)(2,1)}), bf16[128,3,4,128]{3,2,1,0:T(4,128)(2,1)S(1)}, u32[]{:S(2)}, u32[]{:S(2)}) %all-to-all-start.2) | async-done | bytes 393248 | tf_op jit(solution)/shard_map/all_to_all | solution.py:556
  43.6 5.0 %all-to-all-start.1 = ((bf16[128,152,128]{2,1,0:T(8,128)(2,1)}), bf16[128,152,128]{2,1,0:T(8,128)(2,1)}, u32[]{:S(2)}, u32[]{:S(2)}) async-start(bf16[128,152,128]{2,1,0:T(8,128)(2,1)} %pack_field.1), calls=%async_computation.1 | async-start | bytes 9961472 | tf_op jit(solution)/shard_map/all_to_all | solution.py:556
  48.7 1.2 indices.1
  49.9 0.1 reshape.22.idx_ref.idx_any
  50.0 15.0 %near_first.1 = (bf16[16,2048,128]{2,1,0:T(8,128)(2,1)}, f32[16,75,128]{2,1,0:T(8,128)S(1)}) custom-call(s32[640]{0:T(1024)S(1)} %reshape.22.idx_ref.idx_any, bf16[16,75,128]{2,1,0:T(8,128)(2,1)S(1)} %copy.22.field_ref, f32[16,3,128]{2,1,0:T(4,128)S(1)} %copy.23.pos_ref, f32[16,3,128]{2,1,0:T(4,128)S(1)} %copy.24.nrm_ref, f32[16,1,128]{2,1,0:T(1,128)S(1)} %bitcast.4), custom_call_target="tpu_custom_call" | custom-call | flops 600000000 | tf_op jit(solution)/shard_map/near_first/pallas_call | solution.py:331
  65.0 23.2 %far_tiles.1.tiles_ref = bf16[16,3072,128]{2,1,0:T(8,128)(2,1)} custom-call(s32[640]{0:T(1024)S(1)} %reshape.22.idx_ref.idx_any, bf16[128,3,4,128]{3,2,1,0:T(4,128)(2,1)S(1)} %all-to-all-done.2.got_ref, f32[16,3,128]{2,1,0:T(4,128)S(1)} %copy.23.pos_ref, f32[16,3,128]{2,1,0:T(4,128)S(1)} %copy.24.nrm_ref), custom_call_target="tpu_custom_call" | custom-call | flops 600000000 | tf_op jit(solution)/shard_map/far_tiles/pallas_call | solution.py:412
  88.2 20.2 %all-to-all-done.1.got_ref = bf16[128,152,128]{2,1,0:T(8,128)(2,1)} async-done(((bf16[128,152,128]{2,1,0:T(8,128)(2,1)}), bf16[128,152,128]{2,1,0:T(8,128)(2,1)}, u32[]{:S(2)}, u32[]{:S(2)}) %all-to-all-start.1) | async-done | bytes 4980768 | tf_op jit(solution)/shard_map/all_to_all | solution.py:556
  108.4 9.9 %far_bounce_one.1 = (bf16[16,75,128]{2,1,0:T(8,128)(2,1)S(1)}, f32[1,128]{1,0:T(1,128)S(1)}, bf16[128,152,128]{2,1,0:T(8,128)(2,1)}) custom-call(s32[640]{0:T(1024)S(1)} %reshape.22.idx_ref.idx_any, s32[256]{0:T(256)S(1)} %reshape.24.req_ref.req_any, bf16[128,152,128]{2,1,0:T(8,128)(2,1)} %all-to-all-done.1.got_ref, ...), custom_call_target="tpu_custom_call" | custom-call | flops 500000000 | tf_op jit(solution)/shard_map/far_bounce_one/pallas_call | solution.py:526
  118.3 5.8 %all-to-all-start.3 = ((bf16[128,152,128]{2,1,0:T(8,128)(2,1)}), bf16[128,152,128]{2,1,0:T(8,128)(2,1)}, u32[]{:S(2)}, u32[]{:S(2)}) async-start(bf16[128,152,128]{2,1,0:T(8,128)(2,1)} %get-tuple-element.12), calls=%async_computation.3 | async-start | bytes 9961472 | tf_op jit(solution)/shard_map/all_to_all | solution.py:556
  124.1 6.4 %near_again.1.near_ref = f32[16,75,128]{2,1,0:T(8,128)S(1)} custom-call(s32[640]{0:T(1024)S(1)} %reshape.22.idx_ref.idx_any, bf16[16,75,128]{2,1,0:T(8,128)(2,1)S(1)} %get-tuple-element.20.field_ref, bf16[16,2048,128]{2,1,0:T(8,128)(2,1)} %get-tuple-element.13.tiles_ref), custom_call_target="tpu_custom_call" | custom-call | flops 300000000 | tf_op jit(solution)/shard_map/near_again/pallas_call | solution.py:372
  130.5 53.2 %all-to-all-done.3.got_ref = bf16[128,152,128]{2,1,0:T(8,128)(2,1)} async-done(((bf16[128,152,128]{2,1,0:T(8,128)(2,1)}), bf16[128,152,128]{2,1,0:T(8,128)(2,1)}, u32[]{:S(2)}, u32[]{:S(2)}) %all-to-all-start.3) | async-done | bytes 4980768 | tf_op jit(solution)/shard_map/all_to_all | solution.py:556
  183.7 8.3 %far_bounce_two.1 = (bf16[16,75,128]{2,1,0:T(8,128)(2,1)S(1)}, f32[128,2,128]{2,1,0:T(2,128)}) custom-call(s32[640]{0:T(1024)S(1)} %reshape.22.idx_ref.idx_any, s32[256]{0:T(256)S(1)} %reshape.24.req_ref.req_any, bf16[128,152,128]{2,1,0:T(8,128)(2,1)} %all-to-all-done.3.got_ref, bf16[16,3072,128]{2,1,0:T(8,128)(2,1)} %far_tiles.1.tiles_ref, ...), custom_call_target="tpu_custom_call" | custom-call | flops 500000000 | tf_op jit(solution)/shard_map/far_bounce_two/pallas_call | solution.py:526
  192.0 5.4 %all-to-all-start.4 = ((f32[128,2,128]{2,1,0:T(2,128)}), f32[128,2,128]{2,1,0:T(2,128)S(1)}, u32[]{:S(2)}, u32[]{:S(2)}) async-start(f32[128,2,128]{2,1,0:T(2,128)} %get-tuple-element.16), calls=%async_computation.4 | async-start | bytes 262144 | tf_op jit(solution)/shard_map/all_to_all | solution.py:556
  197.4 0.8 copy.32
  198.2 0.8 copy.33
  199.0 8.6 %all-to-all-done.4 = f32[128,2,128]{2,1,0:T(2,128)S(1)} async-done(((f32[128,2,128]{2,1,0:T(2,128)}), f32[128,2,128]{2,1,0:T(2,128)S(1)}, u32[]{:S(2)}, u32[]{:S(2)}) %all-to-all-start.4) | async-done | bytes 131104 | tf_op jit(solution)/shard_map/all_to_all | solution.py:556
  207.6 0.8 reduce_sum.9
  (10 shorter events, 0.1 us)
Async XLA Ops:
  2.4 21.2 %all-to-all-start = ((s32[128,1,2]{2,1,0:T(1,128)}), s32[128,1,2]{2,1,0:T(1,128)S(1)}, u32[]{:S(2)}, u32[]{:S(2)}) async-start(s32[128,1,2]{2,1,0:T(1,128)} %bitcast.1), calls=%async_computation | async-start | bytes 131072 | tf_op jit(solution)/shard_map/all_to_all | solution.py:556
  15.4 0.7 copy-start
  26.5 17.1 %all-to-all-start.2 = ((bf16[128,3,4,128]{3,2,1,0:T(4,128)(2,1)}), bf16[128,3,4,128]{3,2,1,0:T(4,128)(2,1)S(1)}, u32[]{:S(2)}, u32[]{:S(2)}) async-start(bf16[128,3,4,128]{3,2,1,0:T(4,128)(2,1)} %pack_geometry.1), calls=%async_computation.2 | async-start | bytes 786432 | tf_op jit(solution)/shard_map/all_to_all | solution.py:556
  36.2 12.4 %copy-start.4 = (f32[16,3,128]{2,0,1:T(8,128)S(1)}, f32[16,3,128]{2,0,1:T(8,128)}, u32[]{:S(2)}) copy-start(f32[16,3,128]{2,0,1:T(8,128)} %param.11) | copy-start | bytes 73732
  36.2 12.5 %copy-start.2 = (s32[16,40]{1,0:T(8,128)S(1)}, s32[16,40]{1,0:T(8,128)}, u32[]{:S(2)}) copy-start(s32[16,40]{1,0:T(8,128)} %pairs_ref.1) | copy-start | bytes 7684
  36.2 12.5 %copy-start.3 = (s32[2048]{0:T(1024)S(1)}, s32[2048]{0:T(1024)}, u32[]{:S(2)}) copy-start(s32[2048]{0:T(1024)} %param.13) | copy-start | bytes 24580
  36.2 13.8 %copy-start.1 = (f32[16,128]{1,0:T(8,128)S(1)}, f32[16,128]{1,0:T(8,128)}, u32[]{:S(2)}) copy-start(f32[16,128]{1,0:T(8,128)} %param.10) | copy-start | bytes 24580
  43.6 64.8 %all-to-all-start.1 = ((bf16[128,152,128]{2,1,0:T(8,128)(2,1)}), bf16[128,152,128]{2,1,0:T(8,128)(2,1)}, u32[]{:S(2)}, u32[]{:S(2)}) async-start(bf16[128,152,128]{2,1,0:T(8,128)(2,1)} %pack_field.1), calls=%async_computation.1 | async-start | bytes 9961472 | tf_op jit(solution)/shard_map/all_to_all | solution.py:556
  118.3 65.4 %all-to-all-start.3 = ((bf16[128,152,128]{2,1,0:T(8,128)(2,1)}), bf16[128,152,128]{2,1,0:T(8,128)(2,1)}, u32[]{:S(2)}, u32[]{:S(2)}) async-start(bf16[128,152,128]{2,1,0:T(8,128)(2,1)} %get-tuple-element.12), calls=%async_computation.3 | async-start | bytes 9961472 | tf_op jit(solution)/shard_map/all_to_all | solution.py:556
  192.0 15.6 %all-to-all-start.4 = ((f32[128,2,128]{2,1,0:T(2,128)}), f32[128,2,128]{2,1,0:T(2,128)S(1)}, u32[]{:S(2)}, u32[]{:S(2)}) async-start(f32[128,2,128]{2,1,0:T(2,128)} %get-tuple-element.16), calls=%async_computation.4 | async-start | bytes 262144 | tf_op jit(solution)/shard_map/all_to_all | solution.py:556

commit v5 on v4

--- a/solution.py
+++ b/solution.py
@@ -162,24 +162,37 @@
     )(pos, nrm, area)
 
 
-def geometry_kernel(req_ref, table, out_ref):
+def geometry_kernel(asked_ref, table, out_ref, across, req_ref, sem):
+    asked = asked_ref[:, 0, :].astype(F32).astype(BF16)
+    row = lax.broadcasted_iota(I32, (DEVS, DEVS), 0)
+    same = jnp.where(row == lax.broadcasted_iota(I32, (DEVS, DEVS), 1), 1.0, 0.0).astype(BF16)
+    turned = lax.dot_general(asked, same, (((0,), (0,)), ((), ())), preferred_element_type=F32)
+    across[...] = turned.astype(I32)
+    copy = pltpu.make_async_copy(across, req_ref, sem)
+    copy.start()
+    copy.wait()
+
     def put(d, carry):
         for k in range(CAP):
-            out_ref[d, :, 2 * k : 2 * k + 2, :] = table[req_ref[d, 0, k]]
+            out_ref[d, :, 2 * k : 2 * k + 2, :] = table[req_ref[k, d]]
         return carry
 
     lax.fori_loop(0, DEVS, put, 0, unroll=8)
 
 
-def pack_geometry(req, table):
+def pack_geometry(asked, table):
     return pl.pallas_call(
         geometry_kernel,
-        grid_spec=grid_spec(1, 1, [whole(BLK, 3, 2, VERT)], whole(DEVS, 3, 4, VERT), []),
         out_shape=jax.ShapeDtypeStruct((DEVS, 3, 4, VERT), BF16),
+        scratch_shapes=[
+            pltpu.VMEM((CAP, DEVS), I32),
+            pltpu.SMEM((CAP, DEVS), I32),
+            pltpu.SemaphoreType.DMA,
+        ],
         cost_estimate=cost(2e6),
-        compiler_params=params(8),
+        compiler_params=pltpu.CompilerParams(vmem_limit_bytes=8 * 1024 * 1024),
         name="pack_geometry",
-    )(req, table)
+    )(asked, table)
 
 
 def ends(last):

time: 209 us -> 208 us (level)
  no operation moved by 1% of the time
where the time goes in v5:
time: 208 us
  waiting for transfers between devices  96.8 us (47%)
  Pallas kernels  70.8 us (34%)
  starting transfers between devices  32 us (15%)
  local copies, waits for them, and re-layouts  5.62 us (3%)
    all_to_all x5, waiting for transfers between devices, swap(): return lax.all_to_all(value, AXES, split_axis=0, concat_axis=0, tiled=True)  96.8 us
    all_to_all x5, starting transfers between devices, swap(): return lax.all_to_all(value, AXES, split_axis=0, concat_axis=0, tiled=True)  32 us
    pallas_call x1, Pallas kernels, far_tiles(): pl.pallas_call(far_tiles_kernel, grid_spec=grid_spec(1, BLK, [whole(DEVS,...  23.2 us
    pallas_call x2, Pallas kernels, far_bounce(): pl.pallas_call(functools.partial(far_kernel, send=send), grid_spec=grid_s...  18.2 us
    pallas_call x1, Pallas kernels, near_first(): pl.pallas_call(near_kernel, grid_spec=grid_spec(1, BLK, [whole(BLK, CH, V...  15 us
    pallas_call x1, Pallas kernels, near_again(): pl.pallas_call(near_again_kernel, grid_spec=grid_spec(1, BLK, [whole(BLK,...  6.44 us
    unnamed x16, local copies, waits for them, and re-layouts  4.89 us
  transfers between devices with their start and end apart: 5, of which 5 were waited for; matrix products, arithmetic and copies ran while one was open for 3% of the time, Pallas kernels for 23%

profile of v5, /device:TPU:1, one launch (start us, length us, event | category | flops | bytes accessed | tf_op | source)
XLA Modules:
  0.0 207.7 jit_solution(12409333484786331539)
XLA Ops:
  0.6 1.7 requests.1.req_ref
  2.4 11.5 %all-to-all-start = ((s32[128,1,2]{2,1,0:T(1,128)}), s32[128,1,2]{2,1,0:T(1,128)S(1)}, u32[]{:S(2)}, u32[]{:S(2)}) async-start(s32[128,1,2]{2,1,0:T(1,128)} %bitcast.1), calls=%async_computation | async-start | bytes 131072 | tf_op jit(solution)/shard_map/all_to_all | solution.py:569
  13.9 0.8 copy.23.pos_ref
  14.6 0.8 copy.24.nrm_ref
  15.4 0.7 copy-done
  16.1 7.5 %all-to-all-done.asked_ref = s32[128,1,2]{2,1,0:T(1,128)S(1)} async-done(((s32[128,1,2]{2,1,0:T(1,128)}), s32[128,1,2]{2,1,0:T(1,128)S(1)}, u32[]{:S(2)}, u32[]{:S(2)}) %all-to-all-start) | async-done | bytes 1056 | tf_op jit(solution)/shard_map/all_to_all | solution.py:569
  23.6 2.2 %pack_geometry.1 = bf16[128,3,4,128]{3,2,1,0:T(4,128)(2,1)} custom-call(s32[128,1,2]{2,1,0:T(1,128)S(1)} %all-to-all-done.asked_ref, bf16[16,3,2,128]{3,2,1,0:T(2,128)(2,1)S(1)} %source_table.1.table), custom_call_target="tpu_custom_call" | custom-call | flops 2000000 | tf_op jit(solution)/shard_map/pack_geometry/pallas_call | solution.py:184
  25.8 4.3 %all-to-all-start.2 = ((bf16[128,3,4,128]{3,2,1,0:T(4,128)(2,1)}), bf16[128,3,4,128]{3,2,1,0:T(4,128)(2,1)S(1)}, u32[]{:S(2)}, u32[]{:S(2)}) async-start(bf16[128,3,4,128]{3,2,1,0:T(4,128)(2,1)} %pack_geometry.1), calls=%async_computation.2 | async-start | bytes 786432 | tf_op jit(solution)/shard_map/all_to_all | solution.py:569
  30.1 1.1 copy.22.field_ref
  31.1 0.5 broadcast.3
  31.6 0.8 reduce.3
  32.5 0.1 reshape.24.req_ref.req_any
  32.6 2.9 %pack_field.1 = bf16[128,152,128]{2,1,0:T(8,128)(2,1)} custom-call(s32[256]{0:T(256)S(1)} %reshape.24.req_ref.req_any, bf16[16,75,128]{2,1,0:T(8,128)(2,1)S(1)} %copy.22.field_ref), custom_call_target="tpu_custom_call" | custom-call | flops 10000000 | tf_op jit(solution)/shard_map/pack_field/pallas_call | solution.py:246
  35.5 0.0 copy-start.4
  35.5 0.0 copy-start.1
  35.5 7.4 %all-to-all-done.2.got_ref = bf16[128,3,4,128]{3,2,1,0:T(4,128)(2,1)S(1)} async-done(((bf16[128,3,4,128]{3,2,1,0:T(4,128)(2,1)}), bf16[128,3,4,128]{3,2,1,0:T(4,128)(2,1)S(1)}, u32[]{:S(2)}, u32[]{:S(2)}) %all-to-all-start.2) | async-done | bytes 393248 | tf_op jit(solution)/shard_map/all_to_all | solution.py:569
  42.9 5.0 %all-to-all-start.1 = ((bf16[128,152,128]{2,1,0:T(8,128)(2,1)}), bf16[128,152,128]{2,1,0:T(8,128)(2,1)}, u32[]{:S(2)}, u32[]{:S(2)}) async-start(bf16[128,152,128]{2,1,0:T(8,128)(2,1)} %pack_field.1), calls=%async_computation.1 | async-start | bytes 9961472 | tf_op jit(solution)/shard_map/all_to_all | solution.py:569
  48.0 1.2 indices.1
  49.2 0.1 reshape.22.idx_ref.idx_any
  49.3 15.0 %near_first.1 = (bf16[16,2048,128]{2,1,0:T(8,128)(2,1)}, f32[16,75,128]{2,1,0:T(8,128)S(1)}) custom-call(s32[640]{0:T(1024)S(1)} %reshape.22.idx_ref.idx_any, bf16[16,75,128]{2,1,0:T(8,128)(2,1)S(1)} %copy.22.field_ref, f32[16,3,128]{2,1,0:T(4,128)S(1)} %copy.23.pos_ref, f32[16,3,128]{2,1,0:T(4,128)S(1)} %copy.24.nrm_ref, f32[16,1,128]{2,1,0:T(1,128)S(1)} %bitcast.4), custom_call_target="tpu_custom_call" | custom-call | flops 600000000 | tf_op jit(solution)/shard_map/near_first/pallas_call | solution.py:344
  64.3 23.2 %far_tiles.1.tiles_ref = bf16[16,3072,128]{2,1,0:T(8,128)(2,1)} custom-call(s32[640]{0:T(1024)S(1)} %reshape.22.idx_ref.idx_any, bf16[128,3,4,128]{3,2,1,0:T(4,128)(2,1)S(1)} %all-to-all-done.2.got_ref, f32[16,3,128]{2,1,0:T(4,128)S(1)} %copy.23.pos_ref, f32[16,3,128]{2,1,0:T(4,128)S(1)} %copy.24.nrm_ref), custom_call_target="tpu_custom_call" | custom-call | flops 600000000 | tf_op jit(solution)/shard_map/far_tiles/pallas_call | solution.py:425
  87.5 20.2 %all-to-all-done.1.got_ref = bf16[128,152,128]{2,1,0:T(8,128)(2,1)} async-done(((bf16[128,152,128]{2,1,0:T(8,128)(2,1)}), bf16[128,152,128]{2,1,0:T(8,128)(2,1)}, u32[]{:S(2)}, u32[]{:S(2)}) %all-to-all-start.1) | async-done | bytes 4980768 | tf_op jit(solution)/shard_map/all_to_all | solution.py:569
  107.7 9.9 %far_bounce_one.1 = (bf16[16,75,128]{2,1,0:T(8,128)(2,1)S(1)}, f32[1,128]{1,0:T(1,128)S(1)}, bf16[128,152,128]{2,1,0:T(8,128)(2,1)}) custom-call(s32[640]{0:T(1024)S(1)} %reshape.22.idx_ref.idx_any, s32[256]{0:T(256)S(1)} %reshape.24.req_ref.req_any, bf16[128,152,128]{2,1,0:T(8,128)(2,1)} %all-to-all-done.1.got_ref, ...), custom_call_target="tpu_custom_call" | custom-call | flops 500000000 | tf_op jit(solution)/shard_map/far_bounce_one/pallas_call | solution.py:539
  117.6 5.8 %all-to-all-start.3 = ((bf16[128,152,128]{2,1,0:T(8,128)(2,1)}), bf16[128,152,128]{2,1,0:T(8,128)(2,1)}, u32[]{:S(2)}, u32[]{:S(2)}) async-start(bf16[128,152,128]{2,1,0:T(8,128)(2,1)} %get-tuple-element.12), calls=%async_computation.3 | async-start | bytes 9961472 | tf_op jit(solution)/shard_map/all_to_all | solution.py:569
  123.4 6.4 %near_again.1.near_ref = f32[16,75,128]{2,1,0:T(8,128)S(1)} custom-call(s32[640]{0:T(1024)S(1)} %reshape.22.idx_ref.idx_any, bf16[16,75,128]{2,1,0:T(8,128)(2,1)S(1)} %get-tuple-element.20.field_ref, bf16[16,2048,128]{2,1,0:T(8,128)(2,1)} %get-tuple-element.13.tiles_ref), custom_call_target="tpu_custom_call" | custom-call | flops 300000000 | tf_op jit(solution)/shard_map/near_again/pallas_call | solution.py:385
  129.8 53.2 %all-to-all-done.3.got_ref = bf16[128,152,128]{2,1,0:T(8,128)(2,1)} async-done(((bf16[128,152,128]{2,1,0:T(8,128)(2,1)}), bf16[128,152,128]{2,1,0:T(8,128)(2,1)}, u32[]{:S(2)}, u32[]{:S(2)}) %all-to-all-start.3) | async-done | bytes 4980768 | tf_op jit(solution)/shard_map/all_to_all | solution.py:569
  183.0 8.3 %far_bounce_two.1 = (bf16[16,75,128]{2,1,0:T(8,128)(2,1)S(1)}, f32[128,2,128]{2,1,0:T(2,128)}) custom-call(s32[640]{0:T(1024)S(1)} %reshape.22.idx_ref.idx_any, s32[256]{0:T(256)S(1)} %reshape.24.req_ref.req_any, bf16[128,152,128]{2,1,0:T(8,128)(2,1)} %all-to-all-done.3.got_ref, bf16[16,3072,128]{2,1,0:T(8,128)(2,1)} %far_tiles.1.tiles_ref, ...), custom_call_target="tpu_custom_call" | custom-call | flops 500000000 | tf_op jit(solution)/shard_map/far_bounce_two/pallas_call | solution.py:539
  191.3 5.4 %all-to-all-start.4 = ((f32[128,2,128]{2,1,0:T(2,128)}), f32[128,2,128]{2,1,0:T(2,128)S(1)}, u32[]{:S(2)}, u32[]{:S(2)}) async-start(f32[128,2,128]{2,1,0:T(2,128)} %get-tuple-element.16), calls=%async_computation.4 | async-start | bytes 262144 | tf_op jit(solution)/shard_map/all_to_all | solution.py:569
  196.7 0.8 copy.32
  197.5 0.8 copy.33
  198.3 8.6 %all-to-all-done.4 = f32[128,2,128]{2,1,0:T(2,128)S(1)} async-done(((f32[128,2,128]{2,1,0:T(2,128)}), f32[128,2,128]{2,1,0:T(2,128)S(1)}, u32[]{:S(2)}, u32[]{:S(2)}) %all-to-all-start.4) | async-done | bytes 131104 | tf_op jit(solution)/shard_map/all_to_all | solution.py:569
  206.9 0.8 reduce_sum.9
  (10 shorter events, 0.1 us)
Async XLA Ops:
  2.4 21.2 %all-to-all-start = ((s32[128,1,2]{2,1,0:T(1,128)}), s32[128,1,2]{2,1,0:T(1,128)S(1)}, u32[]{:S(2)}, u32[]{:S(2)}) async-start(s32[128,1,2]{2,1,0:T(1,128)} %bitcast.1), calls=%async_computation | async-start | bytes 131072 | tf_op jit(solution)/shard_map/all_to_all | solution.py:569
  15.4 0.7 copy-start
  25.8 17.1 %all-to-all-start.2 = ((bf16[128,3,4,128]{3,2,1,0:T(4,128)(2,1)}), bf16[128,3,4,128]{3,2,1,0:T(4,128)(2,1)S(1)}, u32[]{:S(2)}, u32[]{:S(2)}) async-start(bf16[128,3,4,128]{3,2,1,0:T(4,128)(2,1)} %pack_geometry.1), calls=%async_computation.2 | async-start | bytes 786432 | tf_op jit(solution)/shard_map/all_to_all | solution.py:569
  35.5 12.5 %copy-start.4 = (f32[16,3,128]{2,0,1:T(8,128)S(1)}, f32[16,3,128]{2,0,1:T(8,128)}, u32[]{:S(2)}) copy-start(f32[16,3,128]{2,0,1:T(8,128)} %param.11) | copy-start | bytes 73732
  35.5 12.5 %copy-start.2 = (s32[16,40]{1,0:T(8,128)S(1)}, s32[16,40]{1,0:T(8,128)}, u32[]{:S(2)}) copy-start(s32[16,40]{1,0:T(8,128)} %pairs_ref.1) | copy-start | bytes 7684
  35.5 12.5 %copy-start.3 = (s32[2048]{0:T(1024)S(1)}, s32[2048]{0:T(1024)}, u32[]{:S(2)}) copy-start(s32[2048]{0:T(1024)} %param.13) | copy-start | bytes 24580
  35.5 13.8 %copy-start.1 = (f32[16,128]{1,0:T(8,128)S(1)}, f32[16,128]{1,0:T(8,128)}, u32[]{:S(2)}) copy-start(f32[16,128]{1,0:T(8,128)} %param.10) | copy-start | bytes 24580
  42.9 64.8 %all-to-all-start.1 = ((bf16[128,152,128]{2,1,0:T(8,128)(2,1)}), bf16[128,152,128]{2,1,0:T(8,128)(2,1)}, u32[]{:S(2)}, u32[]{:S(2)}) async-start(bf16[128,152,128]{2,1,0:T(8,128)(2,1)} %pack_field.1), calls=%async_computation.1 | async-start | bytes 9961472 | tf_op jit(solution)/shard_map/all_to_all | solution.py:569
  117.6 65.4 %all-to-all-start.3 = ((bf16[128,152,128]{2,1,0:T(8,128)(2,1)}), bf16[128,152,128]{2,1,0:T(8,128)(2,1)}, u32[]{:S(2)}, u32[]{:S(2)}) async-start(bf16[128,152,128]{2,1,0:T(8,128)(2,1)} %get-tuple-element.12), calls=%async_computation.3 | async-start | bytes 9961472 | tf_op jit(solution)/shard_map/all_to_all | solution.py:569
  191.3 15.6 %all-to-all-start.4 = ((f32[128,2,128]{2,1,0:T(2,128)}), f32[128,2,128]{2,1,0:T(2,128)S(1)}, u32[]{:S(2)}, u32[]{:S(2)}) async-start(f32[128,2,128]{2,1,0:T(2,128)} %get-tuple-element.16), calls=%async_computation.4 | async-start | bytes 262144 | tf_op jit(solution)/shard_map/all_to_all | solution.py:569
